TPU v7x, 8 devices: a whole 2x2x1 slice. The times are simulated.
8 devices in a mesh: ep: 8 (over z, y, x, core).
Axes of the slice: x: 2, y: 2, z: 1, core: 2. Of those that a mesh axis runs over, the one named last changes fastest.
Arguments:
- hidden: bfloat16 [16384, 4096], P('ep')
- grad_out: bfloat16 [16384, 4096], P('ep')
- w_router: bfloat16 [4096, 8], replicated
- b_router: float32 [8], replicated
- expert_ids: int32 [16384, 2], P('ep')
- slot_ids: int32 [16384, 2], P('ep')
- w_gate_up: bfloat16 [8, 4096, 2752], P('ep')
- b_gate_up: float32 [8, 2752], P('ep')
- w_down: bfloat16 [8, 1376, 4096], P('ep')
- b_down: float32 [8, 4096], P('ep')
Outputs:
- output 1: bfloat16 [16384, 4096], P('ep')
- output 2: bfloat16 [16384, 4096], P('ep')
- output 3: float32 [4096, 8], replicated
- output 4: float32 [8], replicated
- output 5: float32 [8, 4096, 2752], P('ep')
- output 6: float32 [8, 2752], P('ep')
- output 7: float32 [8, 1376, 4096], P('ep')
- output 8: float32 [8, 4096], P('ep')
All inputs are finite; a program needn't handle non-finite values.
Results may differ from a plain program's by a relative error of at most 0.00836544.
Values are sent between devices in bfloat16 or wider.
A program may use at most 1 GiB of HBM per device.

v0:
```python
import jax
import jax.numpy as jnp
from jax import lax
from jax.sharding import PartitionSpec as P

SWIGLU_LIMIT = 7.0
SWIGLU_ALPHA = 1.702


def swiglu(pre_act):
    col_pairs = pre_act.reshape(pre_act.shape[:-1] + (pre_act.shape[-1] // 2, 2))
    gate_in = jnp.minimum(col_pairs[..., 0], SWIGLU_LIMIT)
    up_in = jnp.clip(col_pairs[..., 1], -SWIGLU_LIMIT, SWIGLU_LIMIT)
    return gate_in * jax.nn.sigmoid(SWIGLU_ALPHA * gate_in) * (up_in + 1.0)


def solution(mesh):
    ep_size = mesh.shape['ep']

    def local_block(hidden, grad_out, w_router, b_router, expert_ids, slot_ids, w_gate_up, b_gate_up, w_down, b_down):
        tok_local, d_model = hidden.shape
        top_k = expert_ids.shape[1]
        experts = w_router.shape[1]
        local_experts = w_gate_up.shape[0]
        capacity = (3 * tok_local * top_k + 2 * experts - 1) // (2 * experts)
        buf_rows = experts * capacity
        copy_count = tok_local * top_k
        dest_row = jnp.where(slot_ids >= 0, expert_ids * capacity + slot_ids, buf_rows)
        src_copy = jnp.full((buf_rows + 1,), copy_count, jnp.int32).at[dest_row.reshape(-1)].set(jnp.arange(copy_count, dtype=jnp.int32))[:buf_rows]
        src_tok = src_copy // top_k
        logits = jnp.dot(hidden, w_router, preferred_element_type=jnp.float32) + b_router
        gate_w = jax.nn.softmax(jnp.take_along_axis(logits, expert_ids, axis=1), axis=-1)

        send_x = jnp.take(hidden, src_tok, axis=0, mode='fill', fill_value=0)
        recv_x = lax.all_to_all(send_x, 'ep', 0, 0, tiled=True).reshape(ep_size, local_experts, capacity, d_model)
        pre_act = jnp.einsum('secd,edf->secf', recv_x, w_gate_up, preferred_element_type=jnp.float32) + b_gate_up[None, :, None, :]
        act_val, act_vjp = jax.vjp(swiglu, pre_act)
        act_bf = act_val.astype(jnp.bfloat16)
        y_rows = (jnp.einsum('secf,efd->secd', act_bf, w_down, preferred_element_type=jnp.float32) + b_down[None, :, None, :]).astype(jnp.bfloat16)
        back_y = lax.all_to_all(y_rows.reshape(buf_rows, d_model), 'ep', 0, 0, tiled=True)
        y_copies = jnp.take(back_y, dest_row, axis=0, mode='fill', fill_value=0)
        block_out = jnp.sum(gate_w[:, :, None] * y_copies, axis=1).astype(jnp.bfloat16)

        gate_grad = jnp.einsum('td,tkd->tk', grad_out, y_copies, preferred_element_type=jnp.float32)
        sel_grad = gate_w * (gate_grad - jnp.sum(gate_w * gate_grad, axis=1, keepdims=True))
        expert_range = jnp.arange(experts, dtype=jnp.int32)
        logit_grad = jnp.sum(jnp.where(expert_ids[:, :, None] == expert_range, sel_grad[:, :, None], 0.0), axis=1).astype(jnp.bfloat16)
        row_gate = jnp.take(gate_w.reshape(-1), src_copy, axis=0, mode='fill', fill_value=0)
        row_grad = jnp.take(grad_out, src_tok, axis=0, mode='fill', fill_value=0)
        send_q = (row_gate[:, None] * row_grad).astype(jnp.bfloat16)
        recv_q = lax.all_to_all(send_q, 'ep', 0, 0, tiled=True).reshape(ep_size, local_experts, capacity, d_model)
        grad_b_down = jnp.sum(recv_q, axis=(0, 2), dtype=jnp.float32)
        grad_w_down = jnp.einsum('secf,secd->efd', act_bf, recv_q, preferred_element_type=jnp.float32)
        act_grad = jnp.einsum('secd,efd->secf', recv_q, w_down, preferred_element_type=jnp.float32)
        pre_grad = act_vjp(act_grad)[0].astype(jnp.bfloat16)
        grad_b_gate_up = jnp.sum(pre_grad, axis=(0, 2), dtype=jnp.float32)
        grad_w_gate_up = jnp.einsum('secd,secf->edf', recv_x, pre_grad, preferred_element_type=jnp.float32)
        p_rows = jnp.einsum('secf,edf->secd', pre_grad, w_gate_up, preferred_element_type=jnp.float32).astype(jnp.bfloat16)
        back_p = lax.all_to_all(p_rows.reshape(buf_rows, d_model), 'ep', 0, 0, tiled=True)
        p_copies = jnp.take(back_p, dest_row, axis=0, mode='fill', fill_value=0)
        router_dx = jnp.einsum('te,de->td', logit_grad, w_router, preferred_element_type=jnp.float32)
        grad_hidden = (jnp.sum(p_copies, axis=1, dtype=jnp.float32) + router_dx).astype(jnp.bfloat16)
        grad_w_router = lax.psum(jnp.einsum('td,te->de', hidden, logit_grad, preferred_element_type=jnp.float32), 'ep')
        grad_b_router = lax.psum(jnp.sum(logit_grad, axis=0, dtype=jnp.float32), 'ep')
        return (block_out, grad_hidden, grad_w_router, grad_b_router, grad_w_gate_up, grad_b_gate_up, grad_w_down, grad_b_down)

    tok_spec = P('ep', None)
    in_specs = (tok_spec, tok_spec, P(None, None), P(None), tok_spec, tok_spec, P('ep', None, None), P('ep', None), P('ep', None, None), P('ep', None))
    out_specs = (tok_spec, tok_spec, P(None, None), P(None), P('ep', None, None), P('ep', None), P('ep', None, None), P('ep', None))
    return jax.shard_map(local_block, mesh=mesh, in_specs=in_specs, out_specs=out_specs, check_vma=False)
```

profile of v0, /device:TPU:3, one launch (start us, length us, event | category | flops | bytes accessed | tf_op | source)
XLA Modules:
  0.0 4065.1 jit_solution(11269902954529811075)
XLA Ops:
  7.2 0.0 copy-start
  7.2 1.4 compare_and_fusion
  8.6 0.4 copy.79
  9.0 0.6 reshape.397
  9.6 15.6 scatter_custom_fusion
  25.2 0.0 copy-start.7
  25.2 0.6 fusion.46
  25.9 90.9 %gather_fusion.2 = bf16[6144,4096]{1,0:T(8,128)(2,1)} fusion(bf16[2048,4096]{1,0:T(8,128)(2,1)} %param.14, s32[6144]{0:T(1024)S(1)} %get-tuple-element.23), kind=kCustom, calls=%fused_computation.clone | custom fusion | bytes 100687872 | tf_op jit(solution)/shard_map/jit(_take)/gather | solution.py:34
  116.8 33.3 broadcast_select_fusion.2
  150.1 7.5 all-to-all-start
  157.7 541.3 %all-to-all-done = bf16[8,768,4096]{2,1,0:T(8,128)(2,1)} async-done(((bf16[8,768,4096]{2,1,0:T(8,128)(2,1)}), bf16[8,768,4096]{2,1,0:T(8,128)(2,1)}, u32[]{:S(2)}, u32[]{:S(2)}) %all-to-all-start) | async-done | bytes 50331680 | tf_op jit(solution)/shard_map/all_to_all | solution.py:35
  699.0 152.9 %fusion.1 = f32[8,1,768,2752]{2,3,0,1:T(8,128)} fusion(f32[2752]{0:T(1024)S(1)} %reduce.5, bf16[8,768,4096]{2,1,0:T(8,128)(2,1)} %all-to-all-done, bf16[1,4096,2752]{1,2,0:T(8,128)(2,1)} %param.20), kind=kOutput, calls=%fused_computation.12 | convolution fusion | flops 138529603584 | bytes 140520192 | tf_op jit(solution)/shard_map/secd,edf->secf/dot_general | solution.py:36
  851.9 77.3 %reshape.399 = f32[8,1,768,1376,2]{2,4,3,0,1:T(2,128)} reshape(f32[8,1,768,2752]{2,3,0,1:T(8,128)} %fusion.1) | data formatting | bytes 135266304 | tf_op jit(solution)/shard_map/jvp()/reshape | solution.py:11
  929.2 64.8 %fusion.66 = (f32[8,1,768,1376,1]{2,4,3,0,1:T(1,128)}, f32[8,1,768,1376,1]{2,4,3,0,1:T(1,128)}) fusion(f32[8,1,768,1376,2]{2,4,3,0,1:T(2,128)} %reshape.399), kind=kLoop, calls=%fused_computation.118 | loop fusion | bytes 135266304 | tf_op jit(solution)/shard_map/jvp()/slice | solution.py:13
  994.0 103.0 %fusion.2 = bf16[8,768,4096]{2,1,0:T(8,128)(2,1)} fusion(f32[4096]{0:T(1024)S(1)} %bitcast.171, f32[8,1,768,1376,1]{2,4,3,0,1:T(1,128)} %get-tuple-element.21, f32[8,1,768,1376,1]{2,4,3,0,1:T(1,128)} %get-tuple-element.20, bf16[1,1376,4096]{2,1,0:T(8,128)(2,1)} %param.22), kind=kOutput, calls=%fused_computation.20 | convolution fusion | flops 69391220736 | bytes 129253376 | tf_op jit(solution)/shard_map/secf,efd->secd/dot_general | solution.py:39
  1097.0 0.0 copy-start.28
  1097.0 10.3 all-to-all-start.1
  1107.3 1.1 copy.78
  1108.4 0.4 copy.82
  1108.8 1.1 reshape.469
  1109.9 0.4 copy.75
  1110.3 0.5 reshape.441
  1110.8 10.2 convolution_add_fusion
  1121.0 24.5 gather_fusion.1
  1145.5 1.0 reshape.444
  1146.5 0.3 copy.76
  1146.9 90.9 %gather_fusion.4 = bf16[6144,4096]{1,0:T(8,128)(2,1)} fusion(bf16[2048,4096]{1,0:T(8,128)(2,1)} %param.15, s32[6144]{0:T(1024)S(1)} %copy-done.13), kind=kCustom, calls=%fused_computation.2.clone | custom fusion | bytes 100687872 | tf_op jit(solution)/shard_map/jit(_take)/gather | solution.py:49
  1237.8 0.0 copy-start.16
  1237.8 0.6 copy-done.16
  1238.4 0.6 fusion.52
  1239.1 409.6 %all-to-all-done.1 = bf16[8,768,4096]{2,1,0:T(8,128)(2,1)} async-done(((bf16[8,768,4096]{2,1,0:T(8,128)(2,1)}), bf16[8,768,4096]{2,1,0:T(8,128)(2,1)}, u32[]{:S(2)}, u32[]{:S(2)}) %all-to-all-start.1) | async-done | bytes 50331680 | tf_op jit(solution)/shard_map/all_to_all | solution.py:40
  1648.7 201.9 %gather_fusion.3 = bf16[4096,4096]{1,0:T(8,128)(2,1)} fusion(bf16[6144,4096]{1,0:T(8,128)(2,1)} %bitcast.16, s32[4096]{0:T(1024)S(1)} %broadcast_clamp_fusion.1), kind=kCustom, calls=%fused_computation.1.clone | custom fusion | bytes 67125248 | tf_op jit(solution)/shard_map/jit(_take)/gather | solution.py:41
  1850.5 53.0 %reshape.472 = bf16[2048,2,4096]{2,1,0:T(2,128)(2,1)} reshape(bf16[4096,4096]{1,0:T(8,128)(2,1)} %gather_fusion.3) | data formatting | bytes 67108864 | tf_op jit(solution)/shard_map/jit(_take)/gather | solution.py:41
  1903.5 0.0 copy-start.18
  1903.5 104.2 %fusion.20 = f32[2048,1,2]{2,1,0:T(1,128)S(1)} fusion(bf16[2048,4096,1]{1,0,2:T(8,128)(2,1)} %bitcast.164, bf16[2048,2,4096]{2,1,0:T(2,128)(2,1)} %reshape.472, pred[2048,2]{1,0:T(8,128)(4,1)S(1)} %copy-done.3), kind=kOutput, calls=%fused_computation.50 | convolution fusion | flops 50331648 | bytes 50352128 | tf_op jit(solution)/shard_map/td,tkd->tk/dot_general | solution.py:44
  2007.8 0.6 copy.91
  2008.4 0.4 copy.77
  2008.8 0.5 div.58
  2009.3 34.3 gather_fusion
  2043.6 33.4 multiply_convert_fusion
  2077.0 7.3 all-to-all-start.2
  2084.3 0.0 all-reduce.4.cloned.1.call-start
  2084.4 0.1 convert_reduce_fusion.3
  2084.5 34.8 fusion.85
  2119.4 518.3 %psum.15 = f32[8]{0:T(128)} all-reduce(f32[8]{0:T(128)S(1)} %convert_reduce_fusion.3), channel_id=1, replica_groups=mesh['ep'=8] {'ep'}, use_global_device_ids=true, to_apply=%region_9.12 | all-reduce | flops 8 | bytes 64 | tf_op jit(solution)/shard_map/psum | solution.py:64
  2637.7 8.7 convolution_bitcast_fusion.1
  2646.4 0.0 all-reduce.4.cloned.1.call-update
  2646.4 123.4 %multiply_reduce_fusion = bf16[2048,4096]{1,0:T(8,128)(2,1)} fusion(f32[2048,2]{1,0:T(8,128)S(1)} %copy.77, bf16[2048,2,4096]{2,1,0:T(2,128)(2,1)} %reshape.472, pred[2048,2]{1,0:T(8,128)(4,1)S(1)} %copy-done.3), kind=kLoop, calls=%fused_computation.16 | loop fusion | flops 58720256 | bytes 50352128 | tf_op jit(solution)/shard_map/reduce_sum | solution.py:42
  2769.8 116.2 %fusion.15 = (f32[8,1,768,1376,1]{2,3,0,4,1:T(8,128)}, f32[8,1,768,1376,1]{2,3,0,4,1:T(8,128)}) fusion(f32[8,1,768,1376,1]{2,4,3,0,1:T(1,128)} %get-tuple-element.20, f32[8,1,768,1376,1]{2,4,3,0,1:T(1,128)} %get-tuple-element.21, bf16[8,768,4096]{2,1,0:T(8,128)(2,1)} %all-to-all-done.2, bf16[1,1376,4096]{2,1,0:T(8,128)(2,1)} %param.22), kind=kOutput, calls=%fused_computation.39 | convolution fusion | flops 69535334400 | bytes 196870144 | tf_op jit(solution)/shard_map/secd,efd->secf/dot_general | solution.py:54
  2885.9 33.7 convert_reduce_fusion.1
  2919.6 47.0 %copy.85 = bf16[8,1,768,1376,2]{2,0,4,3,1:T(8,128)(2,1)} copy(bf16[8,1,768,1376,2]{2,3,0,4,1:T(8,128)(2,1)} %get-tuple-element.11) | data formatting | bytes 67633152 | tf_op jit(solution)/shard_map/convert_element_type | solution.py:55
  2966.6 155.6 %fusion.26 = bf16[8,768,4096]{2,1,0:T(8,128)(2,1)} fusion(bf16[8,768,2752]{1,0,2:T(8,128)(2,1)} %bitcast.167, bf16[1,4096,2752]{1,2,0:T(8,128)(2,1)} %param.20), kind=kOutput, calls=%fused_computation.57 | convolution fusion | flops 138537861120 | bytes 106692608 | tf_op jit(solution)/shard_map/secf,edf->secd/dot_general | solution.py:58
  3122.3 9.4 all-to-all-start.3
  3131.7 80.6 %convolution_bitcast_fusion = f32[1,1376,4096]{2,1,0:T(8,128)} fusion(bf16[8,768,4096]{2,1,0:T(8,128)(2,1)} %all-to-all-done.2, bf16[8,768,1376]{1,2,0:T(8,128)(2,1)} %fusion.85), kind=kOutput, calls=%fused_computation.61 | convolution fusion | flops 69256347648 | bytes 89784320 | tf_op jit(solution)/shard_map/secf,secd->efd/dot_general | solution.py:53
  3212.3 0.3 copy.89
  3212.6 1.0 reduce_sum.83
  3213.6 17.0 convert_reduce_fusion
  3230.6 177.0 %fusion.29 = f32[1,4096,2752]{1,2,0:T(8,128)} fusion(bf16[8,768,4096]{2,1,0:T(8,128)(2,1)} %all-to-all-done, bf16[8,768,2752]{1,0,2:T(8,128)(2,1)} %bitcast.168), kind=kOutput, calls=%fused_computation.58 | convolution fusion | flops 138512695296 | bytes 129236992 | tf_op jit(solution)/shard_map/secd,secf->edf/dot_general | solution.py:57
  3407.6 265.7 %all-to-all-done.3 = bf16[8,768,4096]{2,1,0:T(8,128)(2,1)} async-done(((bf16[8,768,4096]{2,1,0:T(8,128)(2,1)}), bf16[8,768,4096]{2,1,0:T(8,128)(2,1)}, u32[]{:S(2)}, u32[]{:S(2)}) %all-to-all-start.3) | async-done | bytes 50331680 | tf_op jit(solution)/shard_map/all_to_all | solution.py:59
  3673.3 199.8 %gather_fusion.5 = bf16[4096,4096]{1,0:T(8,128)(2,1)} fusion(bf16[6144,4096]{1,0:T(8,128)(2,1)} %bitcast.31, s32[4096]{0:T(1024)S(1)} %copy-done.2), kind=kCustom, calls=%fused_computation.3.clone | custom fusion | bytes 67125248 | tf_op jit(solution)/shard_map/jit(_take)/gather | solution.py:60
  3873.1 53.2 %reshape.478 = bf16[2048,2,4096]{2,1,0:T(2,128)(2,1)} reshape(bf16[4096,4096]{1,0:T(8,128)(2,1)} %gather_fusion.5) | data formatting | bytes 67108864 | tf_op jit(solution)/shard_map/jit(_take)/gather | solution.py:60
  3926.3 113.0 %convert_reduce_fusion.2 = f32[2048,4096]{1,0:T(8,128)} fusion(bf16[2048,2,4096]{2,1,0:T(2,128)(2,1)} %reshape.478, pred[2048,2]{1,0:T(8,128)(4,1)S(1)} %copy-done.4), kind=kLoop, calls=%fused_computation.15 | loop fusion | flops 41943040 | bytes 67112960 | tf_op jit(solution)/shard_map/reduce_sum | solution.py:62
  4039.3 16.9 add_convert_fusion.1
  4056.2 1.6 copy.141
  (68 shorter events, 0.4 us)
Async XLA Ops:
  7.2 1103.6 %copy-start = (bf16[4096,8]{0,1:T(8,128)(2,1)S(1)}, bf16[4096,8]{0,1:T(8,128)(2,1)}, u32[]{:S(2)}) copy-start(bf16[4096,8]{0,1:T(8,128)(2,1)} %param.16) | copy-start | bytes 196612
  8.6 108.2 %copy-start.14 = (s32[2048,2]{0,1:T(2,128)}, s32[2048,2]{0,1:T(2,128)S(1)}, u32[]{:S(2)}) copy-start(s32[2048,2]{0,1:T(2,128)S(1)} %get-tuple-element.15) | copy-start | bytes 49156
  25.2 91.6 %copy-start.7 = (s32[6145]{0:T(1024)}, s32[6145]{0:T(1024)S(1)}, u32[]{:S(2)}) copy-start(s32[6145]{0:T(1024)S(1)} %scatter_custom_fusion) | copy-start | bytes 73744
  25.2 91.5 %copy-start.22 = (pred[6144]{0:T(1024)(128)(4,1)}, pred[6144]{0:T(1024)(128)(4,1)S(1)}, u32[]{:S(2)}) copy-start(pred[6144]{0:T(1024)(128)(4,1)S(1)} %compare_and_fusion.1) | copy-start | bytes 18436
  25.9 90.9 %copy-start.12 = (s32[6144]{0:T(1024)}, s32[6144]{0:T(1024)S(1)}, u32[]{:S(2)}) copy-start(s32[6144]{0:T(1024)S(1)} %get-tuple-element.23) | copy-start | bytes 73732
  150.1 7.6 copy-start.27
  150.1 548.9 %all-to-all-start = ((bf16[8,768,4096]{2,1,0:T(8,128)(2,1)}), bf16[8,768,4096]{2,1,0:T(8,128)(2,1)}, u32[]{:S(2)}, u32[]{:S(2)}) async-start(bf16[8,768,4096]{2,1,0:T(8,128)(2,1)} %bitcast.166), calls=%async_computation | async-start | bytes 100663296 | tf_op jit(solution)/shard_map/all_to_all | solution.py:35
  929.2 64.8 %copy-start.29 = (f32[1,4096]{1,0:T(1,128)S(1)}, f32[1,4096]{1,0:T(1,128)}, u32[]{:S(2)}) copy-start(f32[1,4096]{1,0:T(1,128)} %param.23) | copy-start | bytes 49156
  1097.0 10.4 copy-start.25
  1097.0 11.5 copy-start.15
  1097.0 12.9 copy-start.9
  1097.0 13.8 copy-start.28
  1097.0 551.7 %all-to-all-start.1 = ((bf16[8,768,4096]{2,1,0:T(8,128)(2,1)}), bf16[8,768,4096]{2,1,0:T(8,128)(2,1)}, u32[]{:S(2)}, u32[]{:S(2)}) async-start(bf16[8,768,4096]{2,1,0:T(8,128)(2,1)} %fusion.2), calls=%async_computation.1 | async-start | bytes 100663296 | tf_op jit(solution)/shard_map/all_to_all | solution.py:40
  1121.0 25.9 copy-start.13
  1146.9 90.9 %copy-start.10 = (s32[2048,2]{0,1:T(2,128)S(1)}, s32[2048,2]{0,1:T(2,128)}, u32[]{:S(2)}) copy-start(s32[2048,2]{0,1:T(2,128)} %param.18) | copy-start | bytes 49156
  1146.9 92.2 %copy-start.21 = (s32[4096]{0:T(1024)S(1)}, s32[4096]{0:T(1024)}, u32[]{:S(2)}) copy-start(s32[4096]{0:T(1024)} %reshape.469) | copy-start | bytes 49156
  1237.8 0.6 copy-start.16
  1237.8 1.2 copy-start.19
  1239.1 611.5 %copy-start.1 = (s32[4096]{0:T(1024)}, s32[4096]{0:T(1024)S(1)}, u32[]{:S(2)}) copy-start(s32[4096]{0:T(1024)S(1)} %broadcast_clamp_fusion.1) | copy-start | bytes 49156
  1850.5 53.0 %copy-start.3 = (pred[2048,2]{1,0:T(8,128)(4,1)S(1)}, pred[2048,2]{1,0:T(8,128)(4,1)}, u32[]{:S(2)}) copy-start(pred[2048,2]{1,0:T(8,128)(4,1)} %copy.78) | copy-start | bytes 12292
  1903.5 104.9 %copy-start.17 = (f32[2048,2]{0,1:T(2,128)S(1)}, f32[2048,2]{0,1:T(2,128)}, u32[]{:S(2)}) copy-start(f32[2048,2]{0,1:T(2,128)} %copy-done.16) | copy-start | bytes 49156
  1903.5 104.9 %copy-start.20 = (f32[2048]{0:T(1024)S(1)}, f32[2048]{0:T(1024)}, u32[]{:S(2)}) copy-start(f32[2048]{0:T(1024)} %copy-done.19) | copy-start | bytes 24580
  1903.5 104.9 %copy-start.26 = (f32[2048]{0:T(1024)S(1)}, f32[2048]{0:T(1024)}, u32[]{:S(2)}) copy-start(f32[2048]{0:T(1024)} %fusion.52) | copy-start | bytes 24580
  1903.5 105.8 %copy-start.18 = (s32[6144]{0:T(1024)S(1)}, s32[6144]{0:T(1024)}, u32[]{:S(2)}) copy-start(s32[6144]{0:T(1024)} %get-tuple-element.22) | copy-start | bytes 73732
  1903.5 140.0 %copy-start.8 = (s32[6145]{0:T(1024)S(1)}, s32[6145]{0:T(1024)}, u32[]{:S(2)}) copy-start(s32[6145]{0:T(1024)} %copy-done.7) | copy-start | bytes 73744
  1903.5 140.1 %copy-start.23 = (pred[6144]{0:T(1024)(128)(4,1)S(1)}, pred[6144]{0:T(1024)(128)(4,1)}, u32[]{:S(2)}) copy-start(pred[6144]{0:T(1024)(128)(4,1)} %copy-done.22) | copy-start | bytes 18436
  2077.0 7.4 copy-start.11
  2077.0 692.8 %all-to-all-start.2 = ((bf16[8,768,4096]{2,1,0:T(8,128)(2,1)}), bf16[8,768,4096]{2,1,0:T(8,128)(2,1)}, u32[]{:S(2)}, u32[]{:S(2)}) async-start(bf16[8,768,4096]{2,1,0:T(8,128)(2,1)} %bitcast.165), calls=%async_computation.2 | async-start | bytes 100663296 | tf_op jit(solution)/shard_map/all_to_all | solution.py:51
  2084.3 1971.9 %all-reduce.4.cloned.1.call-start = ((), (), s32[]{:S(2)}) async-start(), calls=%async_computation.4 | async-start | bytes 262144 | tf_op jit(solution)/shard_map/psum | solution.py:63
  2084.4 553.3 %copy-start.5 = (bf16[2048,8]{0,1:T(8,128)(2,1)}, bf16[2048,8]{0,1:T(8,128)(2,1)S(1)}, u32[]{:S(2)}) copy-start(bf16[2048,8]{0,1:T(8,128)(2,1)S(1)} %select_reduce_fusion) | copy-start | bytes 98308
  3122.3 551.0 %all-to-all-start.3 = ((bf16[8,768,4096]{2,1,0:T(8,128)(2,1)}), bf16[8,768,4096]{2,1,0:T(8,128)(2,1)}, u32[]{:S(2)}, u32[]{:S(2)}) async-start(bf16[8,768,4096]{2,1,0:T(8,128)(2,1)} %fusion.26), calls=%async_computation.3 | async-start | bytes 100663296 | tf_op jit(solution)/shard_map/all_to_all | solution.py:59
  3131.7 80.6 %copy-start.24 = (f32[1376,2]{0,1:T(2,128)S(1)}, f32[1376,2]{0,1:T(2,128)}, u32[]{:S(2)}) copy-start(f32[1376,2]{0,1:T(2,128)} %get-tuple-element.10) | copy-start | bytes 33028
  3230.6 442.7 %copy-start.2 = (s32[4096]{0:T(1024)S(1)}, s32[4096]{0:T(1024)}, u32[]{:S(2)}) copy-start(s32[4096]{0:T(1024)} %copy-done.1) | copy-start | bytes 49156
  3873.1 53.2 %copy-start.4 = (pred[2048,2]{1,0:T(8,128)(4,1)S(1)}, pred[2048,2]{1,0:T(8,128)(4,1)}, u32[]{:S(2)}) copy-start(pred[2048,2]{1,0:T(8,128)(4,1)} %copy.78) | copy-start | bytes 12292
  3926.3 113.0 %copy-start.6 = (bf16[2048,8]{0,1:T(8,128)(2,1)S(1)}, bf16[2048,8]{0,1:T(8,128)(2,1)}, u32[]{:S(2)}) copy-start(bf16[2048,8]{0,1:T(8,128)(2,1)} %copy-done.5) | copy-start | bytes 98308
Sparse Core Ops, SparseCore 0:
  2646.5 42.6 all-reduce.3
where the time goes:
time: 4070 us
  waiting for transfers between devices  1220 us (30%)
  local copies, waits for them, and re-layouts  964 us (24%)
  matrix products  925 us (23%)
  blocking collectives  518 us (13%)
  other arithmetic  392 us (10%)
    all_to_all x1, waiting for transfers between devices, local_block(): lax.all_to_all(send_x, 'ep', 0, 0, tiled=True)  541 us
    psum x1, blocking collectives, local_block(): lax.psum(jnp.sum(logit_grad, axis=0, dtype=jnp.float32), 'ep')  518 us
    all_to_all x1, waiting for transfers between devices, local_block(): lax.all_to_all(y_rows.reshape(buf_rows, d_model), 'ep', 0, 0, tiled=True)  410 us
    all_to_all x1, waiting for transfers between devices, local_block(): lax.all_to_all(p_rows.reshape(buf_rows, d_model), 'ep', 0, 0, tiled=True)  266 us
    gather x2, local copies, waits for them, and re-layouts, local_block(): y_copies = jnp.take(back_y, dest_row, axis=0, mode='fill', fill_value=0)  255 us
    gather x2, local copies, waits for them, and re-layouts, local_block(): p_copies = jnp.take(back_p, dest_row, axis=0, mode='fill', fill_value=0)  253 us
    dot_general x1, matrix products, local_block(): jnp.einsum('secd,secf->edf', recv_x, pre_grad, preferred_element_type=jnp...  177 us
    dot_general x1, matrix products, local_block(): jnp.einsum('secf,edf->secd', pre_grad, w_gate_up, preferred_element_type=...  156 us
  transfers between devices with their start and end apart: 5, of which 3 were waited for; matrix products, arithmetic and copies ran while one was open for 32% of the time, Pallas kernels for 0%

commit v1 on v0

v1 whole, which is shorter than its diff:
```python
import jax
import jax.numpy as jnp
from jax import lax
from jax.experimental import pallas as pl
from jax.sharding import PartitionSpec as P

SWIGLU_LIMIT = 7.0
SWIGLU_ALPHA = 1.702
F32 = jnp.float32
BF16 = jnp.bfloat16
ROWS_FIRST = (((0,), (0,)), ((), ()))
COLS_LAST = (((1,), (1,)), ((), ()))


def swiglu(gate, up):
    gate_in = jnp.minimum(gate, SWIGLU_LIMIT)
    up_in = jnp.clip(up, -SWIGLU_LIMIT, SWIGLU_LIMIT)
    return gate_in * jax.nn.sigmoid(SWIGLU_ALPHA * gate_in) * (up_in + 1.0)


def round_up(value, unit):
    return (value + unit - 1) // unit * unit


def add_copies_kernel(first_ref, second_ref, keep_ref, logit_ref, router_ref, *refs):
    out_ref = refs[-1]
    keep = keep_ref[...]
    total = jnp.where(keep[:, 0:1] > 0, first_ref[...].astype(F32), 0.0) + jnp.where(keep[:, 1:2] > 0, second_ref[...].astype(F32), 0.0)
    total += jnp.dot(logit_ref[...], router_ref[...], preferred_element_type=F32)
    out_ref[...] = total.astype(BF16)


def add_copies(first, second, keep, logit_grad, router_t, lo, into):
    rows, cols = first.shape
    d_model = router_t.shape[1]
    experts = router_t.shape[0]
    tm, tn = min(rows, 512), min(cols, 1024)
    base = lo // tn
    args = [first, second, keep, logit_grad, router_t]
    specs = [
        pl.BlockSpec((tm, tn), lambda i, j: (i, j)),
        pl.BlockSpec((tm, tn), lambda i, j: (i, j)),
        pl.BlockSpec((tm, 2), lambda i, j: (i, 0)),
        pl.BlockSpec((tm, experts), lambda i, j: (i, 0)),
        pl.BlockSpec((experts, tn), lambda i, j: (0, j + base)),
    ]
    aliases = {}
    if into is not None:
        args.append(into)
        specs.append(pl.BlockSpec(memory_space=pl.ANY))
        aliases = {5: 0}
    return pl.pallas_call(
        add_copies_kernel,
        out_shape=jax.ShapeDtypeStruct((rows, d_model), BF16),
        grid=(rows // tm, cols // tn),
        in_specs=specs,
        out_specs=pl.BlockSpec((tm, tn), lambda i, j: (i, j + base)),
        input_output_aliases=aliases,
        cost_estimate=pl.CostEstimate(flops=20 * rows * cols, bytes_accessed=6 * rows * cols, transcendentals=0),
    )(*args)


def solution(mesh):
    def block(hidden, grad_out, w_router, b_router, expert_ids, slot_ids, w_gate_up, b_gate_up, w_down, b_down):
        tok_local, d_model = hidden.shape
        top_k = expert_ids.shape[1]
        experts = w_router.shape[1]
        ff2 = w_gate_up.shape[2]
        ff = ff2 // 2
        ffp = round_up(ff, 128)
        capacity = (3 * tok_local * top_k + 2 * experts - 1) // (2 * experts)
        buf_rows = experts * capacity
        copy_count = tok_local * top_k
        x_cuts = (0, round_up(capacity // 6, 8), capacity)
        p_cuts = (0, d_model * 3 // 4, d_model)

        kept = slot_ids >= 0
        dest_row = jnp.where(kept, expert_ids * capacity + slot_ids, buf_rows)
        src_copy = jnp.full((buf_rows + 1,), copy_count, jnp.int32).at[dest_row.reshape(-1)].set(jnp.arange(copy_count, dtype=jnp.int32))[:buf_rows]
        src_tok = jnp.minimum(src_copy // top_k, tok_local - 1)

        src_slots = src_tok.reshape(experts, capacity)
        x_parts = []
        for lo, hi in zip(x_cuts[:-1], x_cuts[1:]):
            idx = src_slots[:, lo:hi].reshape(-1)
            if x_parts:
                idx, _ = lax.optimization_barrier((idx, x_rows))
            x_rows = jnp.take(hidden, idx, axis=0, mode='clip')
            x_parts.append(lax.all_to_all(x_rows.reshape(experts, hi - lo, d_model), 'ep', 0, 0, tiled=True))

        logits = jnp.dot(hidden, w_router, preferred_element_type=F32) + b_router
        expert_range = jnp.arange(experts, dtype=jnp.int32)
        picked = [expert_ids[:, k:k + 1] == expert_range for k in range(top_k)]
        chosen = jnp.stack([jnp.sum(jnp.where(p, logits, 0.0), axis=1) for p in picked], axis=1)
        gate_w = jax.nn.softmax(chosen, axis=-1)

        row_gate = jnp.zeros((buf_rows + 1,), F32).at[dest_row.reshape(-1)].set(gate_w.reshape(-1))[:buf_rows]
        row_grad = jnp.take(grad_out, src_tok, axis=0, mode='clip')
        send_q = (row_gate[:, None] * row_grad.astype(F32)).astype(BF16)

        col = jnp.arange(2 * ffp, dtype=jnp.int32)
        old_col = jnp.where(col < ffp, 2 * col, 2 * (col - ffp) + 1)
        old_col = jnp.where((col % ffp) < ff, old_col, -1)
        pick = (jnp.arange(ff2, dtype=jnp.int32)[:, None] == old_col[None, :]).astype(BF16)
        w_in = jnp.dot(w_gate_up[0], pick, preferred_element_type=F32).astype(BF16)
        b_pair = b_gate_up[0].reshape(ff, 2)
        b_in = jnp.concatenate([jnp.pad(b_pair[:, 0], (0, ffp - ff)), jnp.pad(b_pair[:, 1], (0, ffp - ff))])
        w_out = jnp.pad(w_down[0], ((0, ffp - ff), (0, 0)))

        *x_parts, send_q = lax.optimization_barrier((*x_parts, send_q))
        recv_q = lax.all_to_all(send_q, 'ep', 0, 0, tiled=True)
        recv_x = jnp.concatenate(x_parts, axis=1).reshape(buf_rows, d_model)

        pre_act = jnp.dot(recv_x, w_in, preferred_element_type=F32) + b_in
        act_val, act_vjp = jax.vjp(swiglu, pre_act[:, :ffp], pre_act[:, ffp:])
        act_bf = act_val.astype(BF16)
        y_rows = (jnp.dot(act_bf, w_out, preferred_element_type=F32) + b_down[0]).astype(BF16)
        recv_q, y_rows = lax.optimization_barrier((recv_q, y_rows))
        back_y = lax.all_to_all(y_rows, 'ep', 0, 0, tiled=True)

        act_grad = lax.dot_general(recv_q, w_out, COLS_LAST, preferred_element_type=F32)
        gate_pre, up_pre = act_vjp(act_grad)
        pre_grad_in = jnp.concatenate([gate_pre.astype(BF16), up_pre.astype(BF16)], axis=1)
        p_sends = [lax.dot_general(pre_grad_in, w_in[lo:hi], COLS_LAST, preferred_element_type=F32).astype(BF16) for lo, hi in zip(p_cuts[:-1], p_cuts[1:])]
        pre_grad = lax.dot_general(pre_grad_in, pick, COLS_LAST, preferred_element_type=F32).astype(BF16)
        grad_b_down = jnp.sum(recv_q, axis=0, dtype=F32)
        grad_b_gate_up = jnp.sum(pre_grad, axis=0, dtype=F32)
        grad_w_down = lax.dot_general(act_bf, recv_q, ROWS_FIRST, preferred_element_type=F32)[:ff]
        back_y, p_sends[0], grad_w_down, grad_b_down, pre_grad = lax.optimization_barrier((back_y, p_sends[0], grad_w_down, grad_b_down, pre_grad))
        p_first = lax.all_to_all(p_sends[0], 'ep', 0, 0, tiled=True)
        grad_w_gate_up = lax.dot_general(recv_x, pre_grad, ROWS_FIRST, preferred_element_type=F32)

        def copies_of(buf):
            return [jnp.take(buf, jnp.minimum(dest_row[:, k], buf_rows - 1), axis=0, mode='clip') for k in range(top_k)]

        y_copies = [jnp.where(kept[:, k:k + 1], rows.astype(F32), 0.0) for k, rows in enumerate(copies_of(back_y))]
        block_out = sum(gate_w[:, k:k + 1] * y_copies[k] for k in range(top_k)).astype(BF16)
        gate_grad = jnp.stack([jnp.sum(grad_out.astype(F32) * y, axis=1) for y in y_copies], axis=1)
        sel_grad = gate_w * (gate_grad - jnp.sum(gate_w * gate_grad, axis=1, keepdims=True))
        logit_grad = sum(jnp.where(picked[k], sel_grad[:, k:k + 1], 0.0) for k in range(top_k)).astype(BF16)

        router_part = lax.dot_general(logit_grad, hidden, ROWS_FIRST, preferred_element_type=F32)
        bias_part = jnp.sum(logit_grad, axis=0, dtype=F32)
        part = jnp.concatenate([router_part, jnp.broadcast_to(bias_part[:, None], (experts, 128))], axis=1)
        total = jnp.sum(lax.all_gather(part, 'ep'), axis=0)
        grad_w_router = total[:, :d_model].T
        grad_b_router = total[:, d_model]

        p_first, p_sends[1], block_out, logit_grad, grad_w_gate_up = lax.optimization_barrier((p_first, p_sends[1], block_out, logit_grad, grad_w_gate_up))
        p_last = lax.all_to_all(p_sends[1], 'ep', 0, 0, tiled=True)

        keep = kept.astype(F32)
        router_t = w_router.T
        grad_hidden = None
        for lo, buf in zip(p_cuts, (p_first, p_last)):
            grad_hidden = add_copies(*copies_of(buf), keep, logit_grad, router_t, lo, grad_hidden)
        return (block_out, grad_hidden, grad_w_router, grad_b_router, grad_w_gate_up[None], grad_b_gate_up[None], grad_w_down[None], grad_b_down[None])

    tok_spec = P('ep', None)
    in_specs = (tok_spec, tok_spec, P(None, None), P(None), tok_spec, tok_spec, P('ep', None, None), P('ep', None), P('ep', None, None), P('ep', None))
    out_specs = (tok_spec, tok_spec, P(None, None), P(None), P('ep', None, None), P('ep', None), P('ep', None, None), P('ep', None))
    return jax.shard_map(block, mesh=mesh, in_specs=in_specs, out_specs=out_specs, check_vma=False)
```

time: 4070 us -> 2550 us (0.63); the launches traced: 4070 us -> 2500 us
  blocking collectives: 518 us -> 0 us
  waiting for transfers between devices: 1220 us -> 738 us
  local copies, waits for them, and re-layouts: 964 us -> 555 us
  other arithmetic: 392 us -> 173 us
    all_to_all x4 -> x6, waiting for transfers between devices: 1220 us -> 696 us  [the longest x1 235 us: block(): recv_q = lax.all_to_all(send_q, 'ep', 0, 0, tiled=True)]
    psum x1 -> x0, blocking collectives: 518 us -> none  [local_block(): lax.psum(jnp.sum(logit_grad, axis=0, dtype=jnp.float32), 'ep')]
    gather x12 -> x9, local copies, waits for them, and re-layouts: 751 us -> 514 us  [the longest x6 322 us: copies_of(): jnp.take(buf, jnp.minimum(dest_row[:, k], buf_rows - 1), axis=0, mode='cl...]
    reduce_sum x8 -> x7, other arithmetic: 288 us -> 60.1 us  [the longest x1 28.5 us: block(): jnp.sum(grad_out.astype(F32) * y, axis=1)]
    reshape x2, local copies, waits for them, and re-layouts: 77.9 us -> 0.63 us  [the longest x1 0.62 us: block(): dest_row.reshape(-1)]
    slice x1 -> x9, local copies, waits for them, and re-layouts: 64.8 us -> 3.42 us  [the longest x1 1.5 us: block(): kept[:, k:k + 1]]
    convert_element_type x1 -> x0, local copies, waits for them, and re-layouts: 47 us -> none  [local_block(): pre_grad = act_vjp(act_grad)[0].astype(jnp.bfloat16)]
    all_gather x0 -> x1, waiting for transfers between devices: none -> 42.3 us  [block(): total = jnp.sum(lax.all_gather(part, 'ep'), axis=0)]
  transfers between devices with their start and end apart: 5 -> 7, of which waited for: 3 -> 6; matrix products, arithmetic and copies ran while one was open for 32% -> 59% of each run, Pallas kernels for 0% -> 1%
where the time goes in v1:
time: 2550 us; the launch traced here: 2500 us
  matrix products  952 us (37%)
  waiting for transfers between devices  738 us (29%)
  local copies, waits for them, and re-layouts  555 us (22%)
  other arithmetic  173 us (7%)
  starting transfers between devices  44.3 us (2%)
  Pallas kernels  26.2 us (1%)
    gather x6, local copies, waits for them, and re-layouts, copies_of(): jnp.take(buf, jnp.minimum(dest_row[:, k], buf_rows - 1), axis=0, mode='cl...  322 us
    all_to_all x1, waiting for transfers between devices, block(): recv_q = lax.all_to_all(send_q, 'ep', 0, 0, tiled=True)  235 us
    all_to_all x2, waiting for transfers between devices, block(): lax.all_to_all(x_rows.reshape(experts, hi - lo, d_model), 'ep', 0, 0, til...  217 us
    all_to_all x1, waiting for transfers between devices, block(): back_y = lax.all_to_all(y_rows, 'ep', 0, 0, tiled=True)  173 us
    dot_general x2, matrix products, block(): lax.dot_general(pre_grad_in, w_in[lo:hi], COLS_LAST, preferred_element_ty...  163 us
    dot_general x1, matrix products, block(): pre_act = jnp.dot(recv_x, w_in, preferred_element_type=F32) + b_in  156 us
    dot_general x1, matrix products, block(): lax.dot_general(recv_x, pre_grad, ROWS_FIRST, preferred_element_type=F32)  151 us
    dot_general x1, matrix products, block(): lax.dot_general(recv_q, w_out, COLS_LAST, preferred_element_type=F32)  116 us
  transfers between devices with their start and end apart: 7, of which 6 were waited for; matrix products, arithmetic and copies ran while one was open for 59% of the time, Pallas kernels for 1%

profile of v1, /device:TPU:3, one launch (start us, length us, event | category | flops | bytes accessed | tf_op | source)
XLA Modules:
  0.0 2504.2 jit_solution(4246161288016939726)
XLA Ops:
  7.2 0.7 broadcast_multiply_fusion
  8.3 1.1 copy.30
  9.4 1.2 fusion.52
  10.5 0.7 copy-done.2
  11.4 0.6 reshape.114
  12.1 15.6 scatter_custom_fusion
  27.6 0.6 fusion.30
  28.3 23.0 gather_fusion
  51.3 3.6 all-to-all-start
  55.0 77.3 %gather_fusion.1 = bf16[5120,4096]{1,0:T(8,128)(2,1)} fusion(bf16[2048,4096]{1,0:T(8,128)(2,1)} %param.10, s32[5120]{0:T(1024)S(1)} %broadcast_clamp_fusion), kind=kCustom, calls=%fused_computation.1 | custom fusion | bytes 83906560 | tf_op jit(solution)/shard_map/jit(_take)/gather | solution.py:88
  132.2 15.2 all-to-all-done
  147.5 8.7 all-to-all-start.1
  156.2 0.7 reshape_squeeze.3
  157.0 8.3 select_reduce_fusion
  165.4 0.5 copy-done.5
  166.8 15.7 scatter_custom_fusion.1
  182.5 91.1 %gather_fusion.2 = bf16[6144,4096]{1,0:T(8,128)(2,1)} fusion(bf16[2048,4096]{1,0:T(8,128)(2,1)} %param.11, s32[6144]{0:T(1024)S(1)} %copy-done.27), kind=kCustom, calls=%fused_computation.2 | custom fusion | bytes 100687872 | tf_op jit(solution)/shard_map/jit(_take)/gather | solution.py:98
  273.7 0.6 slice_reduce_fusion.3
  274.3 0.6 select_maximum_fusion
  275.0 1.5 slice_reduce_fusion.1
  276.5 0.9 fusion.21
  277.4 0.6 broadcast_clamp_fusion.1
  278.0 0.6 fusion.54
  278.6 10.3 iota_compare_fusion.1.clone.5
  288.9 10.7 iota_compare_fusion.12
  299.6 33.8 %multiply_convert_fusion = bf16[6144,4096]{1,0:T(8,128)(2,1)} fusion(bf16[6144,4096]{1,0:T(8,128)(2,1)} %gather_fusion.2, f32[6144]{0:T(1024)S(1)} %slice.121), kind=kLoop, calls=%fused_computation.13 | loop fusion | flops 75497472 | bytes 100687872 | tf_op jit(solution)/shard_map/convert_element_type | solution.py:99
  333.4 73.1 %fusion.9 = bf16[2816,4096]{1,0:T(8,128)(2,1)} fusion(bf16[1,4096,2752]{1,2,0:T(8,128)(2,1)} %param.16, pred[2752,2816]{1,0:T(32,128)(4,1)} %iota_compare_fusion.12), kind=kOutput, calls=%fused_computation.41 | convolution fusion | flops 63496519680 | bytes 53362688 | tf_op jit(solution)/shard_map/dot_general | solution.py:105
  406.5 201.8 %all-to-all-done.1 = bf16[8,640,4096]{2,1,0:T(8,128)(2,1)} async-done(((bf16[8,640,4096]{2,1,0:T(8,128)(2,1)}), bf16[8,640,4096]{2,1,0:T(8,128)(2,1)}, u32[]{:S(2)}, u32[]{:S(2)}) %all-to-all-start.1) | async-done | bytes 41943072 | tf_op jit(solution)/shard_map/all_to_all | solution.py:89
  608.3 9.0 all-to-all-start.2
  617.2 33.5 %pad_maximum_fusion = bf16[8,768,4096]{2,1,0:T(8,128)(2,1)} fusion(bf16[8,640,4096]{2,1,0:T(8,128)(2,1)} %all-to-all-done.1, bf16[8,128,4096]{2,1,0:T(8,128)(2,1)} %all-to-all-done), kind=kLoop, calls=%fused_computation.16 | loop fusion | flops 100663296 | bytes 100663296 | tf_op jit(solution)/shard_map/concatenate | solution.py:112
  650.7 156.0 %convolution_add_fusion = f32[6144,2816]{0,1:T(8,128)} fusion(bf16[6144,4096]{1,0:T(8,128)(2,1)} %bitcast.60, bf16[2816,4096]{1,0:T(8,128)(2,1)} %fusion.9, f32[2816]{0:T(1024)S(1)} %copy-done.32), kind=kOutput, calls=%fused_computation.19 | convolution fusion | flops 141751222272 | bytes 142617600 | tf_op jit(solution)/shard_map/dot_general | solution.py:114
  806.8 29.2 %multiply_convert_fusion.2 = bf16[6144,1408]{0,1:T(8,128)(2,1)} fusion(f32[6144,2816]{0,1:T(8,128)} %convolution_add_fusion), kind=kLoop, calls=%fused_computation.27 | loop fusion | flops 86507520 | bytes 86507520 | tf_op jit(solution)/shard_map/convert_element_type | solution.py:116
  835.9 88.2 %add_convert_fusion = bf16[6144,4096]{1,0:T(8,128)(2,1)} fusion(bf16[6144,1408]{0,1:T(8,128)(2,1)} %multiply_convert_fusion.2, f32[4096]{0:T(1024)S(1)} %bitcast.97, bf16[1376,4096]{1,0:T(8,128)(2,1)} %bitcast.95), kind=kOutput, calls=%fused_computation.12 | convolution fusion | flops 70917292032 | bytes 78921728 | tf_op jit(solution)/shard_map/dot_general | solution.py:117
  924.1 235.1 %all-to-all-done.2 = bf16[8,768,4096]{2,1,0:T(8,128)(2,1)} async-done(((bf16[8,768,4096]{2,1,0:T(8,128)(2,1)}), bf16[8,768,4096]{2,1,0:T(8,128)(2,1)}, u32[]{:S(2)}, u32[]{:S(2)}) %all-to-all-start.2) | async-done | bytes 50331680 | tf_op jit(solution)/shard_map/all_to_all | solution.py:111
  1159.2 115.8 %fusion.4 = (bf16[6144,1408]{0,1:T(8,128)(2,1)}, bf16[6144,1408]{0,1:T(8,128)(2,1)}) fusion(f32[6144,2816]{0,1:T(8,128)} %convolution_add_fusion, bf16[6144,4096]{1,0:T(8,128)(2,1)} %bitcast.9, bf16[1376,4096]{1,0:T(8,128)(2,1)} %bitcast.96), kind=kOutput, calls=%fused_computation.24 | convolution fusion | flops 71169736704 | bytes 165412864 | tf_op jit(solution)/shard_map/dot_general | solution.py:121
  1275.0 9.3 all-to-all-start.3
  1284.2 43.3 %convolution_convert_fusion.2 = bf16[6144,1024]{1,0:T(8,128)(2,1)} fusion(bf16[6144,1408]{0,1:T(8,128)(2,1)} %get-tuple-element.53, bf16[6144,1408]{0,1:T(8,128)(2,1)} %get-tuple-element.52, bf16[4096,2816]{0,1:T(8,128)(2,1)} %bitcast.99), kind=kOutput, calls=%fused_computation.48 | convolution fusion | flops 35508977664 | bytes 52953088 | tf_op jit(solution)/shard_map/dot_general | solution.py:124
  1327.5 108.0 %convert_reduce_fusion.1 = (f32[2752]{0:T(1024)}, bf16[6144,2752]{0,1:T(8,128)(2,1)}) fusion(bf16[6144,1408]{0,1:T(8,128)(2,1)} %get-tuple-element.53, bf16[6144,1408]{0,1:T(8,128)(2,1)} %get-tuple-element.52, pred[2752,2816]{1,0:T(32,128)(4,1)} %iota_compare_fusion.1.clone.5), kind=kOutput, calls=%fused_computation.14 | convolution fusion | flops 95347408896 | bytes 76180224 | tf_op jit(solution)/shard_map/dot_general | solution.py:125
  1435.5 17.0 convert_reduce_fusion
  1452.5 80.9 %fusion.12 = f32[1376,4096]{1,0:T(8,128)} fusion(bf16[6144,4096]{1,0:T(8,128)(2,1)} %bitcast.9, bf16[6144,1408]{0,1:T(8,128)(2,1)} %multiply_convert_fusion.2), kind=kOutput, calls=%fused_computation.44 | convolution fusion | flops 69256347648 | bytes 89784320 | tf_op jit(solution)/shard_map/dot_general | solution.py:128
  1533.3 119.7 %convolution_convert_fusion.1 = bf16[6144,3072]{1,0:T(8,128)(2,1)} fusion(bf16[4096,2816]{0,1:T(8,128)(2,1)} %bitcast.100, bf16[6144,1408]{0,1:T(8,128)(2,1)} %get-tuple-element.53, bf16[6144,1408]{0,1:T(8,128)(2,1)} %get-tuple-element.52), kind=kOutput, calls=%fused_computation.32 | convolution fusion | flops 106388520960 | bytes 89653248 | tf_op jit(solution)/shard_map/dot_general | solution.py:124
  1653.1 173.1 %all-to-all-done.3 = bf16[8,768,4096]{2,1,0:T(8,128)(2,1)} async-done(((bf16[8,768,4096]{2,1,0:T(8,128)(2,1)}), bf16[8,768,4096]{2,1,0:T(8,128)(2,1)}, u32[]{:S(2)}, u32[]{:S(2)}) %all-to-all-start.3) | async-done | bytes 50331680 | tf_op jit(solution)/shard_map/all_to_all | solution.py:119
  1826.2 8.3 all-to-all-start.4
  1834.5 66.1 %gather_fusion.4 = bf16[2048,4096]{1,0:T(8,128)(2,1)} fusion(bf16[6144,4096]{1,0:T(8,128)(2,1)} %bitcast.15, s32[2048]{0:T(1024)S(1)} %copy-done.23), kind=kCustom, calls=%fused_computation.4 | custom fusion | bytes 33562624 | tf_op jit(solution)/shard_map/jit(_take)/gather | solution.py:134
  1900.6 86.9 %gather_fusion.3 = bf16[2048,4096]{1,0:T(8,128)(2,1)} fusion(bf16[6144,4096]{1,0:T(8,128)(2,1)} %bitcast.15, s32[2048]{0:T(1024)S(1)} %copy-done.21), kind=kCustom, calls=%fused_computation.3 | custom fusion | bytes 33562624 | tf_op jit(solution)/shard_map/jit(_take)/gather | solution.py:134
  1987.6 28.5 %fusion.6 = (f32[2048]{0:T(1024)S(1)}, f32[2048]{0:T(1024)S(1)}, bf16[2048,4096]{1,0:T(8,128)(2,1)}) fusion(bf16[2048,4096]{1,0:T(8,128)(2,1)} %param.11, bf16[2048,4096]{1,0:T(8,128)(2,1)} %gather_fusion.3, pred[2048]{0:T(1024)(128)(4,1)S(1)} %copy-done.35, bf16[2048,4096]{1,0:T(8,128)(2,1)} %gather_fusion.4, pred[2048]{0:T(1024)(128)(4,1)S(1)} %copy-done.36, ...), kind=kLoop, calls=%fused_computation.33 | loop fusion | flops 109047808 | bytes 67145728 | tf_op jit(solution)/shard_map/reduce_sum | solution.py:138
  2016.2 0.6 copy-done.17
  2016.8 2.9 convert_reduce_fusion.2
  2019.8 150.9 %fusion.56 = f32[4096,2752]{0,1:T(8,128)} fusion(bf16[6144,2752]{0,1:T(8,128)(2,1)} %get-tuple-element.32, bf16[6144,4096]{1,0:T(8,128)(2,1)} %bitcast.61), kind=kOutput, calls=%fused_computation.136 | convolution fusion | flops 138512695296 | bytes 129236992 | tf_op jit(solution)/shard_map/dot_general | solution.py:131
  2170.7 71.0 %all-to-all-done.4 = bf16[8,768,3072]{2,1,0:T(8,128)(2,1)} async-done(((bf16[8,768,3072]{2,1,0:T(8,128)(2,1)}), bf16[8,768,3072]{2,1,0:T(8,128)(2,1)}, u32[]{:S(2)}, u32[]{:S(2)}) %all-to-all-start.4) | async-done | bytes 37748768 | tf_op jit(solution)/shard_map/all_to_all | solution.py:130
  2241.6 5.5 all-to-all-start.5
  2247.2 7.9 fusion.51
  2255.2 0.7 pad_maximum_fusion.5
  2255.9 0.6 broadcast_in_dim.133
  2256.5 42.3 %all-gather.3.cloned.1.call-done = f32[64,4224]{1,0:T(8,128)} async-done(((f32[8,4224]{1,0:T(8,128)}), f32[64,4224]{1,0:T(8,128)}) %all-gather.3.cloned.1.call-update) | async-done | bytes 1081360 | tf_op jit(solution)/shard_map/all_gather | solution.py:145
  2298.8 1.3 bitcast_reduce_fusion
  2300.1 0.6 slice_reduce_fusion.4
  2300.7 0.7 slice_bitcast_fusion
  2301.4 78.2 %gather_fusion.7 = bf16[2048,3072]{1,0:T(8,128)(2,1)} fusion(bf16[6144,3072]{1,0:T(8,128)(2,1)} %bitcast.18, s32[2048]{0:T(1024)S(1)} %copy-done.22), kind=kCustom, calls=%fused_computation.7 | custom fusion | bytes 25174016 | tf_op jit(solution)/shard_map/jit(_take)/gather | solution.py:134
  2379.6 56.9 %gather_fusion.8 = bf16[2048,3072]{1,0:T(8,128)(2,1)} fusion(bf16[6144,3072]{1,0:T(8,128)(2,1)} %bitcast.18, s32[2048]{0:T(1024)S(1)} %copy-done.24), kind=kCustom, calls=%fused_computation.8 | custom fusion | bytes 25174016 | tf_op jit(solution)/shard_map/jit(_take)/gather | solution.py:134
  2436.6 19.0 shard_map.161.refs_0_
  2455.5 17.1 gather_fusion.6
  2472.7 17.2 gather_fusion.5
  2489.8 7.2 shard_map.162
  (103 shorter events, 2.0 us)
Async XLA Ops:
  10.5 0.7 copy-start.2
  11.4 39.9 %copy-start = (s32[2048,2]{1,0:T(8,128)}, s32[2048,2]{1,0:T(8,128)S(1)}, u32[]{:S(2)}) copy-start(s32[2048,2]{1,0:T(8,128)S(1)} %add_select_fusion) | copy-start | bytes 49156
  12.1 16.2 copy-start.31
  51.3 96.2 %all-to-all-start = ((bf16[8,128,4096]{2,1,0:T(8,128)(2,1)}), bf16[8,128,4096]{2,1,0:T(8,128)(2,1)}, u32[]{:S(2)}, u32[]{:S(2)}) async-start(bf16[8,128,4096]{2,1,0:T(8,128)(2,1)} %bitcast.64), calls=%async_computation | async-start | bytes 16777216 | tf_op jit(solution)/shard_map/all_to_all | solution.py:89
  147.5 8.7 copy-start.34
  147.5 9.4 copy-start.28
  147.5 9.5 copy-start.4
  147.5 9.5 copy-start.39
  147.5 35.0 %copy-start.27 = (s32[6144]{0:T(1024)S(1)}, s32[6144]{0:T(1024)}, u32[]{:S(2)}) copy-start(s32[6144]{0:T(1024)} %get-tuple-element.57) | copy-start | bytes 73732
  147.5 460.7 %all-to-all-start.1 = ((bf16[8,640,4096]{2,1,0:T(8,128)(2,1)}), bf16[8,640,4096]{2,1,0:T(8,128)(2,1)}, u32[]{:S(2)}, u32[]{:S(2)}) async-start(bf16[8,640,4096]{2,1,0:T(8,128)(2,1)} %bitcast.59), calls=%async_computation.1 | async-start | bytes 83886080 | tf_op jit(solution)/shard_map/all_to_all | solution.py:89
  156.9 8.3 copy-start.11
  156.9 8.4 copy-start.14
  165.2 0.6 copy-start.5
  165.3 0.6 copy-start.7
  165.3 0.6 copy-start.9
  165.9 16.6 copy-start.25
  182.5 92.5 %copy-start.3 = (pred[2048,2]{1,0:T(8,128)(4,1)S(1)}, pred[2048,2]{1,0:T(8,128)(4,1)}, u32[]{:S(2)}) copy-start(pred[2048,2]{1,0:T(8,128)(4,1)} %copy-done.2) | copy-start | bytes 12292
  182.5 93.9 %copy-start.1 = (s32[2048,2]{1,0:T(8,128)S(1)}, s32[2048,2]{1,0:T(8,128)}, u32[]{:S(2)}) copy-start(s32[2048,2]{1,0:T(8,128)} %copy-done) | copy-start | bytes 49156
  608.3 550.9 %all-to-all-start.2 = ((bf16[8,768,4096]{2,1,0:T(8,128)(2,1)}), bf16[8,768,4096]{2,1,0:T(8,128)(2,1)}, u32[]{:S(2)}, u32[]{:S(2)}) async-start(bf16[8,768,4096]{2,1,0:T(8,128)(2,1)} %bitcast.58), calls=%async_computation.2 | async-start | bytes 100663296 | tf_op jit(solution)/shard_map/all_to_all | solution.py:111
  617.2 33.5 %copy-start.32 = (f32[2816]{0:T(1024)S(1)}, f32[2816]{0:T(1024)}, u32[]{:S(2)}) copy-start(f32[2816]{0:T(1024)} %select_maximum_fusion) | copy-start | bytes 33796
  806.8 29.2 %copy-start.38 = (f32[1,4096]{1,0:T(1,128)S(1)}, f32[1,4096]{1,0:T(1,128)}, u32[]{:S(2)}) copy-start(f32[1,4096]{1,0:T(1,128)} %param.19) | copy-start | bytes 49156
  1275.0 551.2 %all-to-all-start.3 = ((bf16[8,768,4096]{2,1,0:T(8,128)(2,1)}), bf16[8,768,4096]{2,1,0:T(8,128)(2,1)}, u32[]{:S(2)}, u32[]{:S(2)}) async-start(bf16[8,768,4096]{2,1,0:T(8,128)(2,1)} %bitcast.62), calls=%async_computation.3 | async-start | bytes 100663296 | tf_op jit(solution)/shard_map/all_to_all | solution.py:119
  1826.2 8.3 copy-start.23
  1826.2 415.4 %all-to-all-start.4 = ((bf16[8,768,3072]{2,1,0:T(8,128)(2,1)}), bf16[8,768,3072]{2,1,0:T(8,128)(2,1)}, u32[]{:S(2)}, u32[]{:S(2)}) async-start(bf16[8,768,3072]{2,1,0:T(8,128)(2,1)} %bitcast.63), calls=%async_computation.4 | async-start | bytes 75497472 | tf_op jit(solution)/shard_map/all_to_all | solution.py:130
  1834.5 66.1 %copy-start.21 = (s32[2048]{0:T(1024)S(1)}, s32[2048]{0:T(1024)}, u32[]{:S(2)}) copy-start(s32[2048]{0:T(1024)} %get-tuple-element.68) | copy-start | bytes 24580
  1900.6 86.9 %copy-start.29 = (f32[2048,1]{0,1:T(1,128)S(1)}, f32[2048,1]{0,1:T(1,128)}, u32[]{:S(2)}) copy-start(f32[2048,1]{0,1:T(1,128)} %get-tuple-element.61) | copy-start | bytes 24580
  1900.6 86.9 %copy-start.30 = (f32[2048,1]{0,1:T(1,128)S(1)}, f32[2048,1]{0,1:T(1,128)}, u32[]{:S(2)}) copy-start(f32[2048,1]{0,1:T(1,128)} %get-tuple-element.62) | copy-start | bytes 24580
  1900.6 86.9 %copy-start.35 = (pred[2048]{0:T(1024)(128)(4,1)S(1)}, pred[2048]{0:T(1024)(128)(4,1)}, u32[]{:S(2)}) copy-start(pred[2048]{0:T(1024)(128)(4,1)} %get-tuple-element.48) | copy-start | bytes 6148
  1900.6 86.9 %copy-start.36 = (pred[2048]{0:T(1024)(128)(4,1)S(1)}, pred[2048]{0:T(1024)(128)(4,1)}, u32[]{:S(2)}) copy-start(pred[2048]{0:T(1024)(128)(4,1)} %get-tuple-element.49) | copy-start | bytes 6148
  1987.5 28.5 %copy-start.6 = (f32[2048]{0:T(1024)S(1)}, f32[2048]{0:T(1024)}, u32[]{:S(2)}) copy-start(f32[2048]{0:T(1024)} %copy-done.5) | copy-start | bytes 24580
  1987.5 28.5 %copy-start.8 = (f32[2048]{0:T(1024)S(1)}, f32[2048]{0:T(1024)}, u32[]{:S(2)}) copy-start(f32[2048]{0:T(1024)} %copy-done.7) | copy-start | bytes 24580
  1987.5 28.5 %copy-start.10 = (f32[2048]{0:T(1024)S(1)}, f32[2048]{0:T(1024)}, u32[]{:S(2)}) copy-start(f32[2048]{0:T(1024)} %copy-done.9) | copy-start | bytes 24580
  1987.6 28.5 %copy-start.26 = (f32[2048]{0:T(1024)S(1)}, f32[2048]{0:T(1024)}, u32[]{:S(2)}) copy-start(f32[2048]{0:T(1024)} %copy-done.25) | copy-start | bytes 24580
  1987.6 29.3 %copy-start.12 = (s32[2048,1]{0,1:T(1,128)S(1)}, s32[2048,1]{0,1:T(1,128)}, u32[]{:S(2)}) copy-start(s32[2048,1]{0,1:T(1,128)} %copy-done.11) | copy-start | bytes 24580
  1987.6 29.3 %copy-start.15 = (s32[2048,1]{0,1:T(1,128)S(1)}, s32[2048,1]{0,1:T(1,128)}, u32[]{:S(2)}) copy-start(s32[2048,1]{0,1:T(1,128)} %copy-done.14) | copy-start | bytes 24580
  2016.2 0.6 copy-start.17
  2016.2 0.6 copy-start.19
  2019.8 227.4 %copy-start.13 = (s32[2048,1]{0,1:T(1,128)S(1)}, s32[2048,1]{0,1:T(1,128)}, u32[]{:S(2)}) copy-start(s32[2048,1]{0,1:T(1,128)} %copy-done.11) | copy-start | bytes 24580
  2019.8 227.4 %copy-start.16 = (s32[2048,1]{0,1:T(1,128)S(1)}, s32[2048,1]{0,1:T(1,128)}, u32[]{:S(2)}) copy-start(s32[2048,1]{0,1:T(1,128)} %copy-done.14) | copy-start | bytes 24580
  2019.8 227.4 %copy-start.18 = (f32[2048,1]{0,1:T(1,128)S(1)}, f32[2048,1]{0,1:T(1,128)}, u32[]{:S(2)}) copy-start(f32[2048,1]{0,1:T(1,128)} %copy-done.17) | copy-start | bytes 24580
  2019.8 227.4 %copy-start.20 = (f32[2048,1]{0,1:T(1,128)S(1)}, f32[2048,1]{0,1:T(1,128)}, u32[]{:S(2)}) copy-start(f32[2048,1]{0,1:T(1,128)} %copy-done.19) | copy-start | bytes 24580
  2170.6 84.5 %copy-start.37 = (f32[8]{0:T(128)S(1)}, f32[8]{0:T(128)}, u32[]{:S(2)}) copy-start(f32[8]{0:T(128)} %get-tuple-element.55) | copy-start | bytes 100
  2170.6 85.3 %copy-start.33 = (f32[2752]{0:T(1024)S(1)}, f32[2752]{0:T(1024)}, u32[]{:S(2)}) copy-start(f32[2752]{0:T(1024)} %get-tuple-element.65) | copy-start | bytes 33028
  2170.7 130.8 %copy-start.22 = (s32[2048]{0:T(1024)S(1)}, s32[2048]{0:T(1024)}, u32[]{:S(2)}) copy-start(s32[2048]{0:T(1024)} %get-tuple-element.68) | copy-start | bytes 24580
  2241.6 213.9 %all-to-all-start.5 = ((bf16[8,768,1024]{2,1,0:T(8,128)(2,1)}), bf16[8,768,1024]{2,1,0:T(8,128)(2,1)}, u32[]{:S(2)}, u32[]{:S(2)}) async-start(bf16[8,768,1024]{2,1,0:T(8,128)(2,1)} %bitcast.65), calls=%async_computation.5 | async-start | bytes 25165824 | tf_op jit(solution)/shard_map/all_to_all | solution.py:150
  2247.1 51.7 %all-gather.3.cloned.1.call-start = ((), (), s32[]{:S(2)}) async-start(), calls=%async_computation.6 | async-start | bytes 1216512 | tf_op jit(solution)/shard_map/all_gather | solution.py:145
  2301.4 78.2 %copy-start.24 = (s32[2048]{0:T(1024)S(1)}, s32[2048]{0:T(1024)}, u32[]{:S(2)}) copy-start(s32[2048]{0:T(1024)} %get-tuple-element.67) | copy-start | bytes 24580
Sparse Core Ops, SparseCore 0:
  2256.0 42.7 all-gather.2

commit v2 on v1

--- a/solution.py
+++ b/solution.py
@@ -1,5 +1,6 @@
 import jax
 import jax.numpy as jnp
+import numpy as np
 from jax import lax
 from jax.experimental import pallas as pl
 from jax.sharding import PartitionSpec as P
@@ -61,6 +62,8 @@
 
 
 def solution(mesh):
+    ep_size = mesh.shape['ep']
+
     def block(hidden, grad_out, w_router, b_router, expert_ids, slot_ids, w_gate_up, b_gate_up, w_down, b_down):
         tok_local, d_model = hidden.shape
         top_k = expert_ids.shape[1]
@@ -70,16 +73,24 @@
         ffp = round_up(ff, 128)
         capacity = (3 * tok_local * top_k + 2 * experts - 1) // (2 * experts)
         buf_rows = experts * capacity
-        copy_count = tok_local * top_k
         x_cuts = (0, round_up(capacity // 6, 8), capacity)
         p_cuts = (0, d_model * 3 // 4, d_model)
 
         kept = slot_ids >= 0
-        dest_row = jnp.where(kept, expert_ids * capacity + slot_ids, buf_rows)
-        src_copy = jnp.full((buf_rows + 1,), copy_count, jnp.int32).at[dest_row.reshape(-1)].set(jnp.arange(copy_count, dtype=jnp.int32))[:buf_rows]
-        src_tok = jnp.minimum(src_copy // top_k, tok_local - 1)
+        expert_range = jnp.arange(experts, dtype=jnp.int32)
+        picked = [expert_ids[:, k:k + 1] == expert_range for k in range(top_k)]
+        token = np.arange(tok_local, dtype=np.int32)
+        src_copy = 0
+        for k in range(top_k):
+            number = (jnp.arange(tok_local, dtype=jnp.int32) * top_k + (k + 1))[:, None]
+            digits = jnp.concatenate([jnp.where(picked[k], number >> 6, 0), jnp.where(picked[k], number & 63, 0)], axis=1).astype(BF16)
+            in_slot = (slot_ids[:, k:k + 1] == jnp.arange(capacity, dtype=jnp.int32)).astype(BF16)
+            src_copy += lax.dot_general(digits, in_slot, ROWS_FIRST, preferred_element_type=F32)
+        src_copy = (src_copy[:experts] * 64.0 + src_copy[experts:]).astype(jnp.int32)
+        spread = (np.arange(buf_rows, dtype=np.int32) % tok_local).reshape(experts, capacity)
+        src_slots = jnp.where(src_copy > 0, (src_copy - 1) // top_k, spread)
+        dest_row = expert_ids * capacity + jnp.where(kept, slot_ids, (token % capacity)[:, None])
 
-        src_slots = src_tok.reshape(experts, capacity)
         x_parts = []
         for lo, hi in zip(x_cuts[:-1], x_cuts[1:]):
             idx = src_slots[:, lo:hi].reshape(-1)
@@ -89,13 +100,12 @@
             x_parts.append(lax.all_to_all(x_rows.reshape(experts, hi - lo, d_model), 'ep', 0, 0, tiled=True))
 
         logits = jnp.dot(hidden, w_router, preferred_element_type=F32) + b_router
-        expert_range = jnp.arange(experts, dtype=jnp.int32)
-        picked = [expert_ids[:, k:k + 1] == expert_range for k in range(top_k)]
         chosen = jnp.stack([jnp.sum(jnp.where(p, logits, 0.0), axis=1) for p in picked], axis=1)
         gate_w = jax.nn.softmax(chosen, axis=-1)
 
-        row_gate = jnp.zeros((buf_rows + 1,), F32).at[dest_row.reshape(-1)].set(gate_w.reshape(-1))[:buf_rows]
-        row_grad = jnp.take(grad_out, src_tok, axis=0, mode='clip')
+        gate_row = jnp.where(kept, dest_row, buf_rows)
+        row_gate = jnp.zeros((buf_rows + 1,), F32).at[gate_row.reshape(-1)].set(gate_w.reshape(-1))[:buf_rows]
+        row_grad = jnp.take(grad_out, src_slots.reshape(-1), axis=0, mode='clip')
         send_q = (row_gate[:, None] * row_grad.astype(F32)).astype(BF16)
 
         col = jnp.arange(2 * ffp, dtype=jnp.int32)
@@ -124,14 +134,14 @@
         p_sends = [lax.dot_general(pre_grad_in, w_in[lo:hi], COLS_LAST, preferred_element_type=F32).astype(BF16) for lo, hi in zip(p_cuts[:-1], p_cuts[1:])]
         pre_grad = lax.dot_general(pre_grad_in, pick, COLS_LAST, preferred_element_type=F32).astype(BF16)
         grad_b_down = jnp.sum(recv_q, axis=0, dtype=F32)
+        grad_w_down = lax.dot_general(act_bf, recv_q, ROWS_FIRST, preferred_element_type=F32)[:ff]
         grad_b_gate_up = jnp.sum(pre_grad, axis=0, dtype=F32)
-        grad_w_down = lax.dot_general(act_bf, recv_q, ROWS_FIRST, preferred_element_type=F32)[:ff]
         back_y, p_sends[0], grad_w_down, grad_b_down, pre_grad = lax.optimization_barrier((back_y, p_sends[0], grad_w_down, grad_b_down, pre_grad))
         p_first = lax.all_to_all(p_sends[0], 'ep', 0, 0, tiled=True)
         grad_w_gate_up = lax.dot_general(recv_x, pre_grad, ROWS_FIRST, preferred_element_type=F32)
 
         def copies_of(buf):
-            return [jnp.take(buf, jnp.minimum(dest_row[:, k], buf_rows - 1), axis=0, mode='clip') for k in range(top_k)]
+            return [jnp.take(buf, dest_row[:, k], axis=0, mode='clip') for k in range(top_k)]
 
         y_copies = [jnp.where(kept[:, k:k + 1], rows.astype(F32), 0.0) for k, rows in enumerate(copies_of(back_y))]
         block_out = sum(gate_w[:, k:k + 1] * y_copies[k] for k in range(top_k)).astype(BF16)
@@ -139,21 +149,25 @@
         sel_grad = gate_w * (gate_grad - jnp.sum(gate_w * gate_grad, axis=1, keepdims=True))
         logit_grad = sum(jnp.where(picked[k], sel_grad[:, k:k + 1], 0.0) for k in range(top_k)).astype(BF16)
 
+        piece = d_model // ep_size
         router_part = lax.dot_general(logit_grad, hidden, ROWS_FIRST, preferred_element_type=F32)
         bias_part = jnp.sum(logit_grad, axis=0, dtype=F32)
-        part = jnp.concatenate([router_part, jnp.broadcast_to(bias_part[:, None], (experts, 128))], axis=1)
-        total = jnp.sum(lax.all_gather(part, 'ep'), axis=0)
-        grad_w_router = total[:, :d_model].T
-        grad_b_router = total[:, d_model]
+        part = jnp.concatenate([router_part.reshape(experts, ep_size, piece).swapaxes(0, 1), jnp.broadcast_to(bias_part[None, :, None], (ep_size, experts, 128))], axis=2)
 
-        p_first, p_sends[1], block_out, logit_grad, grad_w_gate_up = lax.optimization_barrier((p_first, p_sends[1], block_out, logit_grad, grad_w_gate_up))
+        p_first, p_sends[1], block_out, logit_grad, grad_w_gate_up, part = lax.optimization_barrier((p_first, p_sends[1], block_out, logit_grad, grad_w_gate_up, part))
         p_last = lax.all_to_all(p_sends[1], 'ep', 0, 0, tiled=True)
+
+        part = lax.all_to_all(part, 'ep', 0, 0, tiled=True)
+        mine = jnp.sum(part, axis=0)
+        pieces = lax.all_to_all(jnp.broadcast_to(mine, (ep_size, experts, piece + 128)), 'ep', 0, 0, tiled=True)
+        grad_w_router = pieces[:, :, :piece].swapaxes(0, 1).reshape(experts, d_model).T
+        grad_b_router = pieces[0, :, piece]
 
         keep = kept.astype(F32)
         router_t = w_router.T
-        grad_hidden = None
-        for lo, buf in zip(p_cuts, (p_first, p_last)):
-            grad_hidden = add_copies(*copies_of(buf), keep, logit_grad, router_t, lo, grad_hidden)
+        grad_hidden = add_copies(*copies_of(p_first), keep, logit_grad, router_t, p_cuts[0], None)
+        last_copies = copies_of(p_last)
+        grad_hidden = add_copies(*last_copies, keep, logit_grad, router_t, p_cuts[1], grad_hidden)
         return (block_out, grad_hidden, grad_w_router, grad_b_router, grad_w_gate_up[None], grad_b_gate_up[None], grad_w_down[None], grad_b_down[None])
 
     tok_spec = P('ep', None)

time: 2550 us -> 2610 us (1.024); the launches traced: 2500 us -> 2590 us
  waiting for transfers between devices: 738 us -> 877 us
  local copies, waits for them, and re-layouts: 555 us -> 501 us
    all_to_all x1, waiting for transfers between devices: 71 us -> 256 us  [block(): p_first = lax.all_to_all(p_sends[0], 'ep', 0, 0, tiled=True)]
    gather x7, local copies, waits for them, and re-layouts: 414 us -> 371 us  [the longest x6 280 us: copies_of(): jnp.take(buf, dest_row[:, k], axis=0, mode='clip')]
    all_gather x1 -> x0, waiting for transfers between devices: 42.3 us -> none  [block(): total = jnp.sum(lax.all_gather(part, 'ep'), axis=0)]
  transfers between devices with their start and end apart: 7 -> 6, of which waited for: 6 -> 6; matrix products, arithmetic and copies ran while one was open for 59% -> 49% of each run, Pallas kernels for 1% -> 1%
where the time goes in v2:
time: 2610 us; the launch traced here: 2590 us
  matrix products  954 us (37%)
  waiting for transfers between devices  877 us (34%)
  local copies, waits for them, and re-layouts  501 us (19%)
  other arithmetic  174 us (7%)
  starting transfers between devices  44.1 us (2%)
  Pallas kernels  26.2 us (1%)
    gather x6, local copies, waits for them, and re-layouts, copies_of(): jnp.take(buf, dest_row[:, k], axis=0, mode='clip')  280 us
    all_to_all x1, waiting for transfers between devices, block(): p_first = lax.all_to_all(p_sends[0], 'ep', 0, 0, tiled=True)  256 us
    all_to_all x1, waiting for transfers between devices, block(): recv_q = lax.all_to_all(send_q, 'ep', 0, 0, tiled=True)  235 us
    all_to_all x2, waiting for transfers between devices, block(): lax.all_to_all(x_rows.reshape(experts, hi - lo, d_model), 'ep', 0, 0, til...  210 us
    all_to_all x1, waiting for transfers between devices, block(): back_y = lax.all_to_all(y_rows, 'ep', 0, 0, tiled=True)  173 us
    dot_general x2, matrix products, block(): lax.dot_general(pre_grad_in, w_in[lo:hi], COLS_LAST, preferred_element_ty...  163 us
    dot_general x1, matrix products, block(): pre_act = jnp.dot(recv_x, w_in, preferred_element_type=F32) + b_in  156 us
    dot_general x1, matrix products, block(): lax.dot_general(recv_x, pre_grad, ROWS_FIRST, preferred_element_type=F32)  151 us
  transfers between devices with their start and end apart: 6, of which 6 were waited for; matrix products, arithmetic and copies ran while one was open for 49% of the time, Pallas kernels for 1%

profile of v2, /device:TPU:3, one launch (start us, length us, event | category | flops | bytes accessed | tf_op | source)
XLA Modules:
  0.0 2591.5 jit_solution(1520399075909671697)
XLA Ops:
  0.7 0.8 fusion.71
  1.5 0.8 fusion.72
  2.3 0.9 fusion.28
  3.8 0.9 fusion.26
  5.3 1.2 fusion.19
  6.6 1.2 fusion.24
  7.8 0.8 fusion.40
  8.6 23.0 gather_fusion
  31.6 4.1 all-to-all-start
  35.7 77.3 %gather_fusion.1 = bf16[5120,4096]{1,0:T(8,128)(2,1)} fusion(bf16[2048,4096]{1,0:T(8,128)(2,1)} %param.12, s32[5120]{0:T(1024)S(1)} %broadcast_clamp_fusion.1), kind=kCustom, calls=%fused_computation.1 | custom fusion | bytes 83906560 | tf_op jit(solution)/shard_map/jit(_take)/gather | solution.py:99
  113.0 15.2 all-to-all-done
  128.2 8.2 all-to-all-start.1
  136.9 0.7 reshape_squeeze.3
  137.6 8.3 select_reduce_fusion
  147.4 1.3 copy.60
  148.7 1.2 fusion.68
  149.9 2.3 broadcast_select_fusion
  152.2 1.8 reshape.142
  154.1 15.6 scatter_custom_fusion
  169.7 91.1 %gather_fusion.2 = bf16[6144,4096]{1,0:T(8,128)(2,1)} fusion(bf16[2048,4096]{1,0:T(8,128)(2,1)} %param.13, s32[6144]{0:T(1024)S(1)} %broadcast_clamp_fusion), kind=kCustom, calls=%fused_computation.2 | custom fusion | bytes 100687872 | tf_op jit(solution)/shard_map/jit(_take)/gather | solution.py:108
  260.8 0.6 slice_reduce_fusion.5
  262.0 1.5 slice_reduce_fusion.3
  263.5 0.9 slice_reduce_fusion.1
  264.4 0.6 broadcast_clamp_fusion.2
  265.6 10.3 iota_compare_fusion.1.clone.5
  276.0 10.7 iota_compare_fusion.18
  286.7 33.9 %multiply_convert_fusion = bf16[6144,4096]{1,0:T(8,128)(2,1)} fusion(bf16[6144,4096]{1,0:T(8,128)(2,1)} %gather_fusion.2, f32[6144]{0:T(1024)S(1)} %slice.131), kind=kLoop, calls=%fused_computation.12 | loop fusion | flops 75497472 | bytes 100687872 | tf_op jit(solution)/shard_map/convert_element_type | solution.py:109
  320.6 73.1 %fusion.9 = bf16[2816,4096]{1,0:T(8,128)(2,1)} fusion(bf16[1,4096,2752]{1,2,0:T(8,128)(2,1)} %param.18, pred[2752,2816]{1,0:T(32,128)(4,1)} %iota_compare_fusion.18), kind=kOutput, calls=%fused_computation.40 | convolution fusion | flops 63496519680 | bytes 53362688 | tf_op jit(solution)/shard_map/dot_general | solution.py:115
  393.6 194.9 %all-to-all-done.1 = bf16[8,640,4096]{2,1,0:T(8,128)(2,1)} async-done(((bf16[8,640,4096]{2,1,0:T(8,128)(2,1)}), bf16[8,640,4096]{2,1,0:T(8,128)(2,1)}, u32[]{:S(2)}, u32[]{:S(2)}) %all-to-all-start.1) | async-done | bytes 41943072 | tf_op jit(solution)/shard_map/all_to_all | solution.py:100
  588.6 9.0 all-to-all-start.2
  597.5 33.5 %pad_maximum_fusion = bf16[8,768,4096]{2,1,0:T(8,128)(2,1)} fusion(bf16[8,640,4096]{2,1,0:T(8,128)(2,1)} %all-to-all-done.1, bf16[8,128,4096]{2,1,0:T(8,128)(2,1)} %all-to-all-done), kind=kLoop, calls=%fused_computation.15 | loop fusion | flops 100663296 | bytes 100663296 | tf_op jit(solution)/shard_map/concatenate | solution.py:122
  631.1 156.0 %convolution_add_fusion = f32[6144,2816]{0,1:T(8,128)} fusion(bf16[6144,4096]{1,0:T(8,128)(2,1)} %bitcast.65, bf16[2816,4096]{1,0:T(8,128)(2,1)} %fusion.9, f32[2816]{0:T(1024)S(1)} %copy-done.24), kind=kOutput, calls=%fused_computation.18 | convolution fusion | flops 141751222272 | bytes 142617600 | tf_op jit(solution)/shard_map/dot_general | solution.py:124
  787.0 29.2 %multiply_convert_fusion.2 = bf16[6144,1408]{0,1:T(8,128)(2,1)} fusion(f32[6144,2816]{0,1:T(8,128)} %convolution_add_fusion), kind=kLoop, calls=%fused_computation.26 | loop fusion | flops 86507520 | bytes 86507520 | tf_op jit(solution)/shard_map/convert_element_type | solution.py:126
  816.2 88.1 %add_convert_fusion = bf16[6144,4096]{1,0:T(8,128)(2,1)} fusion(bf16[6144,1408]{0,1:T(8,128)(2,1)} %multiply_convert_fusion.2, f32[4096]{0:T(1024)S(1)} %bitcast.107, bf16[1376,4096]{1,0:T(8,128)(2,1)} %bitcast.105), kind=kOutput, calls=%fused_computation.11 | convolution fusion | flops 70917292032 | bytes 78921728 | tf_op jit(solution)/shard_map/dot_general | solution.py:127
  904.4 235.1 %all-to-all-done.2 = bf16[8,768,4096]{2,1,0:T(8,128)(2,1)} async-done(((bf16[8,768,4096]{2,1,0:T(8,128)(2,1)}), bf16[8,768,4096]{2,1,0:T(8,128)(2,1)}, u32[]{:S(2)}, u32[]{:S(2)}) %all-to-all-start.2) | async-done | bytes 50331680 | tf_op jit(solution)/shard_map/all_to_all | solution.py:121
  1139.5 115.8 %fusion.4 = (bf16[6144,1408]{0,1:T(8,128)(2,1)}, bf16[6144,1408]{0,1:T(8,128)(2,1)}) fusion(f32[6144,2816]{0,1:T(8,128)} %convolution_add_fusion, bf16[6144,4096]{1,0:T(8,128)(2,1)} %bitcast.11, bf16[1376,4096]{1,0:T(8,128)(2,1)} %bitcast.106), kind=kOutput, calls=%fused_computation.23 | convolution fusion | flops 71169736704 | bytes 165412864 | tf_op jit(solution)/shard_map/dot_general | solution.py:131
  1255.3 9.2 all-to-all-start.3
  1264.5 43.3 %convolution_convert_fusion.2 = bf16[6144,1024]{1,0:T(8,128)(2,1)} fusion(bf16[6144,1408]{0,1:T(8,128)(2,1)} %get-tuple-element.57, bf16[6144,1408]{0,1:T(8,128)(2,1)} %get-tuple-element.56, bf16[4096,2816]{0,1:T(8,128)(2,1)} %bitcast.109), kind=kOutput, calls=%fused_computation.47 | convolution fusion | flops 35508977664 | bytes 52953088 | tf_op jit(solution)/shard_map/dot_general | solution.py:134
  1307.8 108.0 %convert_reduce_fusion.1 = (f32[2752]{0:T(1024)}, bf16[6144,2752]{0,1:T(8,128)(2,1)}) fusion(bf16[6144,1408]{0,1:T(8,128)(2,1)} %get-tuple-element.57, bf16[6144,1408]{0,1:T(8,128)(2,1)} %get-tuple-element.56, pred[2752,2816]{1,0:T(32,128)(4,1)} %iota_compare_fusion.1.clone.5), kind=kOutput, calls=%fused_computation.13 | convolution fusion | flops 95347408896 | bytes 76180224 | tf_op jit(solution)/shard_map/dot_general | solution.py:135
  1415.8 17.0 convert_reduce_fusion
  1432.8 80.8 %fusion.12 = f32[1376,4096]{1,0:T(8,128)} fusion(bf16[6144,4096]{1,0:T(8,128)(2,1)} %bitcast.11, bf16[6144,1408]{0,1:T(8,128)(2,1)} %multiply_convert_fusion.2), kind=kOutput, calls=%fused_computation.43 | convolution fusion | flops 69256347648 | bytes 89784320 | tf_op jit(solution)/shard_map/dot_general | solution.py:137
  1513.6 120.0 %convolution_convert_fusion.1 = bf16[6144,3072]{1,0:T(8,128)(2,1)} fusion(bf16[4096,2816]{0,1:T(8,128)(2,1)} %bitcast.110, bf16[6144,1408]{0,1:T(8,128)(2,1)} %get-tuple-element.57, bf16[6144,1408]{0,1:T(8,128)(2,1)} %get-tuple-element.56), kind=kOutput, calls=%fused_computation.31 | convolution fusion | flops 106388520960 | bytes 89653248 | tf_op jit(solution)/shard_map/dot_general | solution.py:134
  1633.6 172.9 %all-to-all-done.3 = bf16[8,768,4096]{2,1,0:T(8,128)(2,1)} async-done(((bf16[8,768,4096]{2,1,0:T(8,128)(2,1)}), bf16[8,768,4096]{2,1,0:T(8,128)(2,1)}, u32[]{:S(2)}, u32[]{:S(2)}) %all-to-all-start.3) | async-done | bytes 50331680 | tf_op jit(solution)/shard_map/all_to_all | solution.py:129
  1806.5 66.1 %gather_fusion.4 = bf16[2048,4096]{1,0:T(8,128)(2,1)} fusion(bf16[6144,4096]{1,0:T(8,128)(2,1)} %bitcast.17, s32[2048]{0:T(1024)S(1)} %copy-done.16), kind=kCustom, calls=%fused_computation.4 | custom fusion | bytes 33562624 | tf_op jit(solution)/shard_map/jit(_take)/gather | solution.py:144
  1872.6 66.3 %gather_fusion.3 = bf16[2048,4096]{1,0:T(8,128)(2,1)} fusion(bf16[6144,4096]{1,0:T(8,128)(2,1)} %bitcast.17, s32[2048]{0:T(1024)S(1)} %copy-done.14), kind=kCustom, calls=%fused_computation.3 | custom fusion | bytes 33562624 | tf_op jit(solution)/shard_map/jit(_take)/gather | solution.py:144
  1939.0 28.5 %fusion.6 = (f32[2048]{0:T(1024)S(1)}, f32[2048]{0:T(1024)S(1)}, bf16[2048,4096]{1,0:T(8,128)(2,1)}) fusion(bf16[2048,4096]{1,0:T(8,128)(2,1)} %param.13, bf16[2048,4096]{1,0:T(8,128)(2,1)} %gather_fusion.3, pred[2048]{0:T(1024)(128)(4,1)S(1)} %copy-done.28, bf16[2048,4096]{1,0:T(8,128)(2,1)} %gather_fusion.4, pred[2048]{0:T(1024)(128)(4,1)S(1)} %copy-done.29, ...), kind=kLoop, calls=%fused_computation.32 | loop fusion | flops 109047808 | bytes 67145728 | tf_op jit(solution)/shard_map/reduce_sum | solution.py:148
  1967.6 7.7 fusion.67
  1975.4 2.4 convert_reduce_fusion.2
  1977.8 7.5 all-to-all-start.4
  1985.4 0.7 pad_maximum_fusion.5
  1986.0 150.7 %fusion.73 = f32[4096,2752]{0,1:T(8,128)} fusion(bf16[6144,2752]{0,1:T(8,128)(2,1)} %get-tuple-element.33, bf16[6144,4096]{1,0:T(8,128)(2,1)} %bitcast.66), kind=kOutput, calls=%fused_computation.152 | convolution fusion | flops 138512695296 | bytes 129236992 | tf_op jit(solution)/shard_map/dot_general | solution.py:141
  2136.8 255.7 %all-to-all-done.4 = bf16[8,768,3072]{2,1,0:T(8,128)(2,1)} async-done(((bf16[8,768,3072]{2,1,0:T(8,128)(2,1)}), bf16[8,768,3072]{2,1,0:T(8,128)(2,1)}, u32[]{:S(2)}, u32[]{:S(2)}) %all-to-all-start.4) | async-done | bytes 37748768 | tf_op jit(solution)/shard_map/all_to_all | solution.py:140
  2392.5 6.7 all_to_all.68
  2399.2 7.0 all_to_all.69
  2406.2 6.1 all-to-all-start.5
  2412.9 56.7 %gather_fusion.7 = bf16[2048,3072]{1,0:T(8,128)(2,1)} fusion(bf16[6144,3072]{1,0:T(8,128)(2,1)} %bitcast.20, s32[2048]{0:T(1024)S(1)} %copy-done.15), kind=kCustom, calls=%fused_computation.7 | custom fusion | bytes 25174016 | tf_op jit(solution)/shard_map/jit(_take)/gather | solution.py:144
  2469.6 56.7 %gather_fusion.8 = bf16[2048,3072]{1,0:T(8,128)(2,1)} fusion(bf16[6144,3072]{1,0:T(8,128)(2,1)} %bitcast.20, s32[2048]{0:T(1024)S(1)} %copy-done.17), kind=kCustom, calls=%fused_computation.8 | custom fusion | bytes 25174016 | tf_op jit(solution)/shard_map/jit(_take)/gather | solution.py:144
  2526.4 19.0 shard_map.179.refs_0_
  2545.4 0.7 slice.147
  2546.0 0.6 slice_reduce_fusion.6
  2546.6 3.1 all-to-all-done.5
  2549.8 17.2 gather_fusion.6
  2567.0 17.1 gather_fusion.5
  2584.1 7.2 shard_map.180
  (100 shorter events, 5.4 us)
Async XLA Ops:
  1.5 0.8 copy-start.4
  1.5 30.1 %copy-start.1 = (s32[2048,1]{0,1:T(1,128)}, s32[2048,1]{0,1:T(1,128)S(1)}, u32[]{:S(2)}) copy-start(s32[2048,1]{0,1:T(1,128)S(1)} %get-tuple-element.65) | copy-start | bytes 24580
  31.6 96.6 %all-to-all-start = ((bf16[8,128,4096]{2,1,0:T(8,128)(2,1)}), bf16[8,128,4096]{2,1,0:T(8,128)(2,1)}, u32[]{:S(2)}, u32[]{:S(2)}) async-start(bf16[8,128,4096]{2,1,0:T(8,128)(2,1)} %bitcast.69), calls=%async_computation | async-start | bytes 16777216 | tf_op jit(solution)/shard_map/all_to_all | solution.py:100
  128.2 8.3 copy-start.20
  128.2 8.6 copy-start.26
  128.2 9.4 copy-start.2
  128.2 9.4 copy-start.5
  128.2 9.4 copy-start.7
  128.2 9.4 copy-start.31
  128.2 19.1 copy-start.21
  128.2 460.3 %all-to-all-start.1 = ((bf16[8,640,4096]{2,1,0:T(8,128)(2,1)}), bf16[8,640,4096]{2,1,0:T(8,128)(2,1)}, u32[]{:S(2)}, u32[]{:S(2)}) async-start(bf16[8,640,4096]{2,1,0:T(8,128)(2,1)} %bitcast.64), calls=%async_computation.1 | async-start | bytes 83886080 | tf_op jit(solution)/shard_map/all_to_all | solution.py:100
  136.4 13.5 copy-start.27
  145.8 0.6 copy-start.8
  145.9 0.6 copy-start.10
  145.9 0.6 copy-start.12
  146.5 0.9 copy-start.18
  588.6 550.9 %all-to-all-start.2 = ((bf16[8,768,4096]{2,1,0:T(8,128)(2,1)}), bf16[8,768,4096]{2,1,0:T(8,128)(2,1)}, u32[]{:S(2)}, u32[]{:S(2)}) async-start(bf16[8,768,4096]{2,1,0:T(8,128)(2,1)} %bitcast.63), calls=%async_computation.2 | async-start | bytes 100663296 | tf_op jit(solution)/shard_map/all_to_all | solution.py:121
  597.5 33.5 %copy-start.24 = (f32[2816]{0:T(1024)S(1)}, f32[2816]{0:T(1024)}, u32[]{:S(2)}) copy-start(f32[2816]{0:T(1024)} %select_maximum_fusion) | copy-start | bytes 33796
  787.0 29.2 %copy-start.30 = (f32[1,4096]{1,0:T(1,128)S(1)}, f32[1,4096]{1,0:T(1,128)}, u32[]{:S(2)}) copy-start(f32[1,4096]{1,0:T(1,128)} %param.21) | copy-start | bytes 49156
  1255.3 551.2 %all-to-all-start.3 = ((bf16[8,768,4096]{2,1,0:T(8,128)(2,1)}), bf16[8,768,4096]{2,1,0:T(8,128)(2,1)}, u32[]{:S(2)}, u32[]{:S(2)}) async-start(bf16[8,768,4096]{2,1,0:T(8,128)(2,1)} %bitcast.67), calls=%async_computation.3 | async-start | bytes 100663296 | tf_op jit(solution)/shard_map/all_to_all | solution.py:129
  1513.6 292.9 %copy-start.16 = (s32[2048]{0:T(1024)S(1)}, s32[2048]{0:T(1024)}, u32[]{:S(2)}) copy-start(s32[2048]{0:T(1024)} %get-tuple-element.79) | copy-start | bytes 24580
  1806.5 66.1 %copy-start.14 = (s32[2048]{0:T(1024)S(1)}, s32[2048]{0:T(1024)}, u32[]{:S(2)}) copy-start(s32[2048]{0:T(1024)} %get-tuple-element.80) | copy-start | bytes 24580
  1872.6 66.3 %copy-start.22 = (f32[2048,1]{0,1:T(1,128)S(1)}, f32[2048,1]{0,1:T(1,128)}, u32[]{:S(2)}) copy-start(f32[2048,1]{0,1:T(1,128)} %get-tuple-element.63) | copy-start | bytes 24580
  1872.6 66.3 %copy-start.23 = (f32[2048,1]{0,1:T(1,128)S(1)}, f32[2048,1]{0,1:T(1,128)}, u32[]{:S(2)}) copy-start(f32[2048,1]{0,1:T(1,128)} %get-tuple-element.64) | copy-start | bytes 24580
  1872.6 66.3 %copy-start.28 = (pred[2048]{0:T(1024)(128)(4,1)S(1)}, pred[2048]{0:T(1024)(128)(4,1)}, u32[]{:S(2)}) copy-start(pred[2048]{0:T(1024)(128)(4,1)} %get-tuple-element.50) | copy-start | bytes 6148
  1872.6 66.3 %copy-start.29 = (pred[2048]{0:T(1024)(128)(4,1)S(1)}, pred[2048]{0:T(1024)(128)(4,1)}, u32[]{:S(2)}) copy-start(pred[2048]{0:T(1024)(128)(4,1)} %get-tuple-element.51) | copy-start | bytes 6148
  1938.9 28.5 %copy-start.9 = (f32[2048]{0:T(1024)S(1)}, f32[2048]{0:T(1024)}, u32[]{:S(2)}) copy-start(f32[2048]{0:T(1024)} %copy-done.8) | copy-start | bytes 24580
  1938.9 28.5 %copy-start.11 = (f32[2048]{0:T(1024)S(1)}, f32[2048]{0:T(1024)}, u32[]{:S(2)}) copy-start(f32[2048]{0:T(1024)} %copy-done.10) | copy-start | bytes 24580
  1938.9 28.5 %copy-start.13 = (f32[2048]{0:T(1024)S(1)}, f32[2048]{0:T(1024)}, u32[]{:S(2)}) copy-start(f32[2048]{0:T(1024)} %copy-done.12) | copy-start | bytes 24580
  1939.0 28.5 %copy-start.19 = (f32[2048]{0:T(1024)S(1)}, f32[2048]{0:T(1024)}, u32[]{:S(2)}) copy-start(f32[2048]{0:T(1024)} %copy-done.18) | copy-start | bytes 24580
  1939.0 28.7 %copy-start.3 = (s32[2048,1]{0,1:T(1,128)S(1)}, s32[2048,1]{0,1:T(1,128)}, u32[]{:S(2)}) copy-start(s32[2048,1]{0,1:T(1,128)} %copy-done.1) | copy-start | bytes 24580
  1939.0 28.7 %copy-start.6 = (s32[2048,1]{0,1:T(1,128)S(1)}, s32[2048,1]{0,1:T(1,128)}, u32[]{:S(2)}) copy-start(s32[2048,1]{0,1:T(1,128)} %copy-done.4) | copy-start | bytes 24580
  1977.8 414.6 %all-to-all-start.4 = ((bf16[8,768,3072]{2,1,0:T(8,128)(2,1)}), bf16[8,768,3072]{2,1,0:T(8,128)(2,1)}, u32[]{:S(2)}, u32[]{:S(2)}) async-start(bf16[8,768,3072]{2,1,0:T(8,128)(2,1)} %bitcast.68), calls=%async_computation.4 | async-start | bytes 75497472 | tf_op jit(solution)/shard_map/all_to_all | solution.py:140
  1986.0 406.4 %copy-start = (f32[8,8,640]{2,1,0:T(8,128)S(1)}, f32[8,8,640]{2,1,0:T(8,128)}, u32[]{:S(2)}) copy-start(f32[8,8,640]{2,1,0:T(8,128)} %pad_maximum_fusion.5) | copy-start | bytes 491524
  1986.0 426.3 %copy-start.25 = (f32[2752]{0:T(1024)S(1)}, f32[2752]{0:T(1024)}, u32[]{:S(2)}) copy-start(f32[2752]{0:T(1024)} %get-tuple-element.73) | copy-start | bytes 33028
  1986.0 426.9 %copy-start.15 = (s32[2048]{0:T(1024)S(1)}, s32[2048]{0:T(1024)}, u32[]{:S(2)}) copy-start(s32[2048]{0:T(1024)} %get-tuple-element.80) | copy-start | bytes 24580
  2406.2 143.6 %all-to-all-start.5 = ((bf16[8,768,1024]{2,1,0:T(8,128)(2,1)}), bf16[8,768,1024]{2,1,0:T(8,128)(2,1)}, u32[]{:S(2)}, u32[]{:S(2)}) async-start(bf16[8,768,1024]{2,1,0:T(8,128)(2,1)} %bitcast.70), calls=%async_computation.5 | async-start | bytes 25165824 | tf_op jit(solution)/shard_map/all_to_all | solution.py:158
  2412.9 56.7 %copy-start.17 = (s32[2048]{0:T(1024)S(1)}, s32[2048]{0:T(1024)}, u32[]{:S(2)}) copy-start(s32[2048]{0:T(1024)} %get-tuple-element.79) | copy-start | bytes 24580

commit v3 on v2

--- a/solution.py
+++ b/solution.py
@@ -3,6 +3,7 @@
 import numpy as np
 from jax import lax
 from jax.experimental import pallas as pl
+from jax.experimental.pallas import tpu as pltpu
 from jax.sharding import PartitionSpec as P
 
 SWIGLU_LIMIT = 7.0
@@ -61,6 +62,44 @@
     )(*args)
 
 
+def place_rows_kernel(owners, halves, me_ref, *refs):
+    count = len(owners)
+    pieces, out_ref, buf, in_sem, out_sem = refs[:count], refs[count], refs[count + 1], refs[count + 2], refs[count + 3]
+    slots, lag = buf.shape[0], 2
+    cols = buf.shape[2]
+    me = me_ref[0]
+    ins = [pltpu.make_async_copy(pieces[i], buf.at[i % slots], in_sem.at[i % slots]) for i in range(count)]
+    outs = [
+        pltpu.make_async_copy(buf.at[i % slots], out_ref.at[me ^ owners[i], :, pl.ds(halves[i] * cols, cols)], out_sem.at[i % slots])
+        for i in range(count)
+    ]
+    for i in range(count + lag):
+        if i < count:
+            if i >= slots:
+                outs[i - slots].wait()
+            ins[i].start()
+        if i >= lag:
+            ins[i - lag].wait()
+            outs[i - lag].start()
+    for copy in outs[-slots:]:
+        copy.wait()
+
+
+def place_rows(pieces, owners, halves, me, ep_size):
+    rows, cols = pieces[0].shape
+    slots = 6
+    return pl.pallas_call(
+        lambda *refs: place_rows_kernel(owners, halves, *refs),
+        out_shape=jax.ShapeDtypeStruct((ep_size, rows, 2 * cols), BF16),
+        in_specs=[pl.BlockSpec(memory_space=pltpu.SMEM)] + [pl.BlockSpec(memory_space=pl.ANY)] * len(pieces),
+        out_specs=pl.BlockSpec(memory_space=pl.ANY),
+        scratch_shapes=[pltpu.VMEM((slots, rows, cols), BF16), pltpu.SemaphoreType.DMA((slots,)), pltpu.SemaphoreType.DMA((slots,))],
+        compiler_params=pltpu.CompilerParams(vmem_limit_bytes=slots * rows * cols * 2 + (1 << 20)),
+        cost_estimate=pl.CostEstimate(flops=200_000_000, bytes_accessed=4 * ep_size * rows * 2 * cols, transcendentals=0),
+        name='place_rows',
+    )(me.reshape(1), *pieces)
+
+
 def solution(mesh):
     ep_size = mesh.shape['ep']
 
@@ -73,40 +112,83 @@
         ffp = round_up(ff, 128)
         capacity = (3 * tok_local * top_k + 2 * experts - 1) // (2 * experts)
         buf_rows = experts * capacity
-        x_cuts = (0, round_up(capacity // 6, 8), capacity)
         p_cuts = (0, d_model * 3 // 4, d_model)
+
+        half = d_model // 2
+        me = lax.axis_index('ep')
+
+        def shift(value, mask):
+            return lax.ppermute(value, 'ep', [(d, d ^ mask) for d in range(ep_size)])
+
+        across = (2, 4)
+        targets = ((1, 4, 5, 0), (1, 2, 3, 0))
+        halves_of = lambda array: (array[:, :half], array[:, half:])
+        hidden_halves = halves_of(hidden)
+        hidden_near = [shift(v, m) for v, m in zip(hidden_halves, across)]
+        ids = jnp.concatenate([expert_ids.T, slot_ids.T], axis=0)
+        near_ids = [shift(ids, m) for m in across]
 
         kept = slot_ids >= 0
         expert_range = jnp.arange(experts, dtype=jnp.int32)
         picked = [expert_ids[:, k:k + 1] == expert_range for k in range(top_k)]
         token = np.arange(tok_local, dtype=np.int32)
-        src_copy = 0
-        for k in range(top_k):
-            number = (jnp.arange(tok_local, dtype=jnp.int32) * top_k + (k + 1))[:, None]
-            digits = jnp.concatenate([jnp.where(picked[k], number >> 6, 0), jnp.where(picked[k], number & 63, 0)], axis=1).astype(BF16)
-            in_slot = (slot_ids[:, k:k + 1] == jnp.arange(capacity, dtype=jnp.int32)).astype(BF16)
-            src_copy += lax.dot_general(digits, in_slot, ROWS_FIRST, preferred_element_type=F32)
-        src_copy = (src_copy[:experts] * 64.0 + src_copy[experts:]).astype(jnp.int32)
         spread = (np.arange(buf_rows, dtype=np.int32) % tok_local).reshape(experts, capacity)
-        src_slots = jnp.where(src_copy > 0, (src_copy - 1) // top_k, spread)
         dest_row = expert_ids * capacity + jnp.where(kept, slot_ids, (token % capacity)[:, None])
 
-        x_parts = []
-        for lo, hi in zip(x_cuts[:-1], x_cuts[1:]):
-            idx = src_slots[:, lo:hi].reshape(-1)
-            if x_parts:
-                idx, _ = lax.optimization_barrier((idx, x_rows))
-            x_rows = jnp.take(hidden, idx, axis=0, mode='clip')
-            x_parts.append(lax.all_to_all(x_rows.reshape(experts, hi - lo, d_model), 'ep', 0, 0, tiled=True))
+        def source_of(owner_ids):
+            table = 0
+            for k in range(top_k):
+                number = (jnp.arange(tok_local, dtype=jnp.int32) * top_k + (k + 1))[None, :]
+                hit = (owner_ids[k:k + 1] ^ me) == expert_range[:, None]
+                digits = jnp.concatenate([jnp.where(hit, number >> 6, 0), jnp.where(hit, number & 63, 0)], axis=0).astype(BF16)
+                in_slot = (owner_ids[top_k + k:top_k + k + 1] == jnp.arange(capacity, dtype=jnp.int32)[:, None]).astype(BF16)
+                table += lax.dot_general(digits, in_slot, COLS_LAST, preferred_element_type=F32)
+            table = (table[:experts] * 64.0 + table[experts:]).astype(jnp.int32)
+            return jnp.where(table > 0, (table - 1) // top_k, spread)
+
+        def gates_of(owner_ids, gates):
+            slots = owner_ids[top_k:]
+            rows = jnp.where(slots >= 0, (owner_ids[:top_k] ^ me) * capacity + slots, buf_rows)
+            return jnp.zeros((buf_rows + 1,), F32).at[rows.reshape(-1)].set(gates.reshape(-1))[:buf_rows].reshape(experts, capacity)
+
+        own_source = source_of(ids)
+        near_source = [source_of(i) for i in near_ids]
+
+        def rows_for(h, values, source, gates):
+            got = []
+            for m in targets[h]:
+                rows = jnp.take(values, source[m], axis=0, mode='clip')
+                if gates is not None:
+                    rows = (gates[m][:, None] * rows.astype(F32)).astype(BF16)
+                if m:
+                    rows = shift(rows, m)
+                got.append(rows)
+            return got
+
+        def dispatch(own_values, near_values, own_gates, near_gates):
+            pieces, owners, halves = [], [], []
+            for h in range(2):
+                pieces += rows_for(h, own_values[h], own_source, own_gates)
+                owners += targets[h]
+                halves += [h] * len(targets[h])
+            for h in range(2):
+                pieces += rows_for(h, near_values[h], near_source[h], near_gates and near_gates[h])
+                owners += [m ^ across[h] for m in targets[h]]
+                halves += [h] * len(targets[h])
+            return place_rows(pieces, owners, halves, me, ep_size).reshape(buf_rows, d_model)
+
+        recv_x = dispatch(hidden_halves, hidden_near, None, None)
 
         logits = jnp.dot(hidden, w_router, preferred_element_type=F32) + b_router
         chosen = jnp.stack([jnp.sum(jnp.where(p, logits, 0.0), axis=1) for p in picked], axis=1)
         gate_w = jax.nn.softmax(chosen, axis=-1)
-
-        gate_row = jnp.where(kept, dest_row, buf_rows)
-        row_gate = jnp.zeros((buf_rows + 1,), F32).at[gate_row.reshape(-1)].set(gate_w.reshape(-1))[:buf_rows]
-        row_grad = jnp.take(grad_out, src_slots.reshape(-1), axis=0, mode='clip')
-        send_q = (row_gate[:, None] * row_grad.astype(F32)).astype(BF16)
+        gate_t = gate_w.T
+        near_gate_t = [shift(gate_t, m) for m in across]
+        own_gates = gates_of(ids, gate_t)
+        near_gates = [gates_of(i, g) for i, g in zip(near_ids, near_gate_t)]
+        grad_halves = halves_of(grad_out)
+        grad_near = [shift(v, m) for v, m in zip(grad_halves, across)]
+        recv_q = dispatch(grad_halves, grad_near, own_gates, near_gates)
 
         col = jnp.arange(2 * ffp, dtype=jnp.int32)
         old_col = jnp.where(col < ffp, 2 * col, 2 * (col - ffp) + 1)
@@ -117,17 +199,13 @@
         b_in = jnp.concatenate([jnp.pad(b_pair[:, 0], (0, ffp - ff)), jnp.pad(b_pair[:, 1], (0, ffp - ff))])
         w_out = jnp.pad(w_down[0], ((0, ffp - ff), (0, 0)))
 
-        *x_parts, send_q = lax.optimization_barrier((*x_parts, send_q))
-        recv_q = lax.all_to_all(send_q, 'ep', 0, 0, tiled=True)
-        recv_x = jnp.concatenate(x_parts, axis=1).reshape(buf_rows, d_model)
-
         pre_act = jnp.dot(recv_x, w_in, preferred_element_type=F32) + b_in
-        act_val, act_vjp = jax.vjp(swiglu, pre_act[:, :ffp], pre_act[:, ffp:])
-        act_bf = act_val.astype(BF16)
+        act_bf = swiglu(pre_act[:, :ffp], pre_act[:, ffp:]).astype(BF16)
         y_rows = (jnp.dot(act_bf, w_out, preferred_element_type=F32) + b_down[0]).astype(BF16)
-        recv_q, y_rows = lax.optimization_barrier((recv_q, y_rows))
         back_y = lax.all_to_all(y_rows, 'ep', 0, 0, tiled=True)
 
+        recv_q, pre_act = lax.optimization_barrier((recv_q, pre_act))
+        _, act_vjp = jax.vjp(swiglu, pre_act[:, :ffp], pre_act[:, ffp:])
         act_grad = lax.dot_general(recv_q, w_out, COLS_LAST, preferred_element_type=F32)
         gate_pre, up_pre = act_vjp(act_grad)
         pre_grad_in = jnp.concatenate([gate_pre.astype(BF16), up_pre.astype(BF16)], axis=1)

time: 2610 us -> 2980 us (1.14)
  local copies, waits for them, and re-layouts: 501 us -> 735 us
  waiting for transfers between devices: 877 us -> 954 us
  Pallas kernels: 26.2 us -> 89.4 us
    all_to_all x3 -> x0, waiting for transfers between devices: 445 us -> none  [the longest x1 235 us: block(): recv_q = lax.all_to_all(send_q, 'ep', 0, 0, tiled=True)]
    ppermute x0 -> x32, waiting for transfers between devices: none -> 438 us  [shift(): return lax.ppermute(value, 'ep', [(d, d ^ mask) for d in range(ep_size)])]
    gather x3 -> x32, local copies, waits for them, and re-layouts: 191 us -> 372 us  [rows_for(): rows = jnp.take(values, source[m], axis=0, mode='clip')]
    all_to_all x1, waiting for transfers between devices: 173 us -> 257 us  [block(): back_y = lax.all_to_all(y_rows, 'ep', 0, 0, tiled=True)]
    pallas_call x0 -> x2, Pallas kernels: none -> 63.2 us  [place_rows(): pl.pallas_call(lambda *refs: place_rows_kernel(owners, halves, *refs), ou...]
    concatenate x1, other arithmetic: 33.5 us -> 0.63 us  [block(): ids = jnp.concatenate([expert_ids.T, slot_ids.T], axis=0)]
    scatter x1 -> x3, local copies, waits for them, and re-layouts: 15.6 us -> 47.2 us  [gates_of(): jnp.zeros((buf_rows + 1,), F32).at[rows.reshape(-1)].set(gates.reshape(-1))]
    convert_element_type x2 -> x15, other arithmetic: 63.1 us -> 73.2 us  [the longest x14 44.7 us: rows_for(): rows = (gates[m][:, None] * rows.astype(F32)).astype(BF16)]
  transfers between devices with their start and end apart: 6 -> 35, of which waited for: 6 -> 8; matrix products, arithmetic and copies ran while one was open for 49% -> 45% of each run, Pallas kernels for 1% -> 2%
where the time goes in v3:
time: 2980 us; the launch traced here: 2970 us
  matrix products  978 us (33%)
  waiting for transfers between devices  954 us (32%)
  local copies, waits for them, and re-layouts  735 us (25%)
  other arithmetic  149 us (5%)
  Pallas kernels  89.4 us (3%)
  starting transfers between devices  49 us (2%)
    ppermute x32, waiting for transfers between devices, shift(): return lax.ppermute(value, 'ep', [(d, d ^ mask) for d in range(ep_size)])  438 us
    gather x32, local copies, waits for them, and re-layouts, rows_for(): rows = jnp.take(values, source[m], axis=0, mode='clip')  372 us
    gather x6, local copies, waits for them, and re-layouts, copies_of(): jnp.take(buf, dest_row[:, k], axis=0, mode='clip')  280 us
    all_to_all x1, waiting for transfers between devices, block(): back_y = lax.all_to_all(y_rows, 'ep', 0, 0, tiled=True)  257 us
    all_to_all x1, waiting for transfers between devices, block(): p_first = lax.all_to_all(p_sends[0], 'ep', 0, 0, tiled=True)  256 us
    dot_general x1, matrix products, block(): pre_act = jnp.dot(recv_x, w_in, preferred_element_type=F32) + b_in  170 us
    dot_general x2, matrix products, block(): lax.dot_general(pre_grad_in, w_in[lo:hi], COLS_LAST, preferred_element_ty...  160 us
    dot_general x1, matrix products, block(): lax.dot_general(recv_x, pre_grad, ROWS_FIRST, preferred_element_type=F32)  151 us
  transfers between devices with their start and end apart: 35, of which 8 were waited for; matrix products, arithmetic and copies ran while one was open for 45% of the time, Pallas kernels for 2%

profile of v3, /device:TPU:3, one launch (start us, length us, event | category | flops | bytes accessed | tf_op | source)
XLA Modules:
  0.0 2970.6 jit_solution(7262928137222509002)
XLA Ops:
  26.6 15.7 scatter_custom_fusion
  55.2 12.2 fusion.111
  68.1 72.7 %fusion.11 = bf16[2816,4096]{1,0:T(8,128)(2,1)} fusion(bf16[1,4096,2752]{1,2,0:T(8,128)(2,1)} %param.18, pred[2752,2816]{1,0:T(32,128)(4,1)S(1)} %iota_compare_fusion.36), kind=kOutput, calls=%fused_computation.70 | convolution fusion | flops 63496519680 | bytes 53362688 | tf_op jit(solution)/shard_map/dot_general | solution.py:197
  150.2 11.6 gather_fusion
  166.8 11.8 gather_fusion.4
  190.3 11.8 gather_fusion.1
  205.6 11.5 gather_fusion.5
  217.1 11.6 gather_fusion.2
  230.1 219.9 %collective-permute-done.1.refs_2_ = bf16[768,2048]{1,0:T(8,128)(2,1)} collective-permute-done((bf16[768,2048]{1,0:T(8,128)(2,1)}, bf16[768,2048]{1,0:T(8,128)(2,1)}, u32[]{:S(2)}, u32[]{:S(2)}) %collective-permute-start.1) | collective-permute-done | bytes 3145760 | tf_op jit(solution)/shard_map/ppermute | solution.py:121
  454.0 11.9 gather_fusion.21
  466.0 11.6 gather_fusion.20
  477.5 11.6 gather_fusion.23
  489.1 11.5 gather_fusion.19
  500.6 11.7 gather_fusion.18
  512.4 11.5 gather_fusion.17
  523.9 11.6 gather_fusion.16
  535.5 11.8 gather_fusion.22
  547.3 11.5 gather_fusion.6
  558.8 11.6 gather_fusion.7
  570.4 11.5 gather_fusion.3
  581.9 15.5 scatter_custom_fusion.2
  597.5 16.0 scatter_custom_fusion.1
  624.6 11.6 gather_fusion.14
  636.1 11.5 gather_fusion.13
  647.7 11.7 gather_fusion.12
  676.1 11.6 gather_fusion.30
  687.6 11.6 gather_fusion.28
  699.2 11.8 gather_fusion.31
  711.0 11.6 gather_fusion.10
  722.7 11.5 gather_fusion.9
  734.2 12.0 gather_fusion.8
  753.6 44.3 %collective-permute-done.14.refs_14_ = bf16[768,2048]{1,0:T(8,128)(2,1)} collective-permute-done((bf16[768,2048]{1,0:T(8,128)(2,1)}, bf16[768,2048]{1,0:T(8,128)(2,1)}, u32[]{:S(2)}, u32[]{:S(2)}) %collective-permute-start.14) | collective-permute-done | bytes 3145760 | tf_op jit(solution)/shard_map/ppermute | solution.py:121
  799.0 67.2 %collective-permute-done.15.refs_15_ = bf16[768,2048]{1,0:T(8,128)(2,1)} collective-permute-done((bf16[768,2048]{1,0:T(8,128)(2,1)}, bf16[768,2048]{1,0:T(8,128)(2,1)}, u32[]{:S(2)}, u32[]{:S(2)}) %collective-permute-start.15) | collective-permute-done | bytes 3145760 | tf_op jit(solution)/shard_map/ppermute | solution.py:121
  869.0 11.6 gather_fusion.29
  880.6 11.5 gather_fusion.26
  892.1 11.7 gather_fusion.25
  903.9 11.6 gather_fusion.24
  915.4 11.6 gather_fusion.15
  927.0 11.6 gather_fusion.27
  938.6 11.6 gather_fusion.11
  968.5 31.4 %place_rows.2 = bf16[8,768,4096]{2,1,0:T(8,128)(2,1)} custom-call(s32[1]{0:T(128)} %bitcast.refs_0_, bf16[768,2048]{1,0:T(8,128)(2,1)S(1)} %copy-done.4, bf16[768,2048]{1,0:T(8,128)(2,1)} %collective-permute-done.1.refs_2_, bf16[768,2048]{1,0:T(8,128)(2,1)S(1)} %copy-done.6, bf16[768,2048]{1,0:T(8,128)(2,1)S(1)} %copy-done.2, ...), custom_call_target="tpu_custom_call" | custom-call | flops 200000000 | bytes 100663296 | tf_op jit(solution)/shard_map/place_rows/pallas_call | solution.py:91
  1001.2 169.8 %convolution_add_fusion = f32[6144,2816]{1,0:T(8,128)} fusion(bf16[6144,4096]{1,0:T(8,128)(2,1)} %bitcast.103, bf16[2816,4096]{1,0:T(8,128)(2,1)} %fusion.11, f32[2816]{0:T(1024)S(1)} %copy-done.58), kind=kOutput, calls=%fused_computation.47 | convolution fusion | flops 141751222272 | bytes 142617600 | tf_op jit(solution)/shard_map/dot_general | solution.py:202
  1174.1 28.6 fusion.7
  1202.7 39.5 %collective-permute-done.31.refs_15_ = bf16[768,2048]{1,0:T(8,128)(2,1)} collective-permute-done((bf16[768,2048]{1,0:T(8,128)(2,1)}, bf16[768,2048]{1,0:T(8,128)(2,1)}, u32[]{:S(2)}, u32[]{:S(2)}) %collective-permute-start.31) | collective-permute-done | bytes 3145760 | tf_op jit(solution)/shard_map/ppermute | solution.py:121
  1242.2 67.3 %collective-permute-done.26.refs_11_ = bf16[768,2048]{1,0:T(8,128)(2,1)} collective-permute-done((bf16[768,2048]{1,0:T(8,128)(2,1)}, bf16[768,2048]{1,0:T(8,128)(2,1)}, u32[]{:S(2)}, u32[]{:S(2)}) %collective-permute-start.26) | collective-permute-done | bytes 3145760 | tf_op jit(solution)/shard_map/ppermute | solution.py:121
  1311.4 31.8 %place_rows.3 = bf16[8,768,4096]{2,1,0:T(8,128)(2,1)} custom-call(s32[1]{0:T(128)} %bitcast.refs_0_, bf16[768,2048]{1,0:T(8,128)(2,1)} %collective-permute-done.16.refs_1_, bf16[768,2048]{1,0:T(8,128)(2,1)} %collective-permute-done.17.refs_2_, bf16[768,2048]{1,0:T(8,128)(2,1)} %collective-permute-done.18.refs_3_, bf16[768,2048]{1,0:T(8,128)(2,1)S(1)} %copy-done, ...), custom_call_target="tpu_custom_call" | custom-call | flops 200000000 | bytes 100663296 | tf_op jit(solution)/shard_map/place_rows/pallas_call | solution.py:91
  1343.2 81.4 %fusion.13 = f32[1376,4096]{1,0:T(8,128)} fusion(bf16[6144,4096]{1,0:T(8,128)(2,1)} %bitcast.99, bf16[6144,1408]{1,0:T(8,128)(2,1)} %fusion.7), kind=kOutput, calls=%fused_computation.72 | convolution fusion | flops 69256347648 | bytes 90177536 | tf_op jit(solution)/shard_map/dot_general | solution.py:215
  1424.6 123.6 %fusion.4 = (bf16[6144,1408]{1,0:T(8,128)(2,1)}, bf16[6144,1408]{1,0:T(8,128)(2,1)}) fusion(f32[6144,2816]{1,0:T(8,128)} %convolution_add_fusion, bf16[6144,4096]{1,0:T(8,128)(2,1)} %bitcast.100, bf16[1376,4096]{1,0:T(8,128)(2,1)} %bitcast.165), kind=kOutput, calls=%fused_computation.52 | convolution fusion | flops 71169736704 | bytes 165412864 | tf_op jit(solution)/shard_map/dot_general | solution.py:209
  1548.2 87.0 %add_convert_fusion = bf16[6144,4096]{1,0:T(8,128)(2,1)} fusion(bf16[6144,1408]{1,0:T(8,128)(2,1)} %fusion.7, f32[4096]{0:T(1024)S(1)} %bitcast.167, bf16[1376,4096]{1,0:T(8,128)(2,1)} %bitcast.166), kind=kOutput, calls=%fused_computation.42 | convolution fusion | flops 70917292032 | bytes 78921728 | tf_op jit(solution)/shard_map/dot_general | solution.py:204
  1643.2 42.4 %convolution_convert_fusion.2 = bf16[6144,1024]{1,0:T(8,128)(2,1)} fusion(bf16[6144,1408]{1,0:T(8,128)(2,1)} %get-tuple-element.61, bf16[6144,1408]{1,0:T(8,128)(2,1)} %get-tuple-element.60, bf16[4096,2816]{0,1:T(8,128)(2,1)} %bitcast.169), kind=kOutput, calls=%fused_computation.77 | convolution fusion | flops 35508977664 | bytes 52953088 | tf_op jit(solution)/shard_map/dot_general | solution.py:212
  1685.6 17.0 convert_reduce_fusion
  1702.6 108.2 %convert_reduce_fusion.1 = (f32[2752]{0:T(1024)}, bf16[6144,2752]{0,1:T(8,128)(2,1)}) fusion(bf16[6144,1408]{1,0:T(8,128)(2,1)} %get-tuple-element.61, bf16[6144,1408]{1,0:T(8,128)(2,1)} %get-tuple-element.60, pred[2752,2816]{1,0:T(32,128)(4,1)} %iota_compare_fusion.1.clone.5), kind=kOutput, calls=%fused_computation.43 | convolution fusion | flops 95347408896 | bytes 76180224 | tf_op jit(solution)/shard_map/dot_general | solution.py:213
  1810.8 117.9 %convolution_convert_fusion.1 = bf16[6144,3072]{1,0:T(8,128)(2,1)} fusion(bf16[4096,2816]{0,1:T(8,128)(2,1)} %bitcast.170, bf16[6144,1408]{1,0:T(8,128)(2,1)} %get-tuple-element.61, bf16[6144,1408]{1,0:T(8,128)(2,1)} %get-tuple-element.60), kind=kOutput, calls=%fused_computation.62 | convolution fusion | flops 106388520960 | bytes 89653248 | tf_op jit(solution)/shard_map/dot_general | solution.py:212
  1928.7 256.5 %all-to-all-done = bf16[8,768,4096]{2,1,0:T(8,128)(2,1)} async-done(((bf16[8,768,4096]{2,1,0:T(8,128)(2,1)}), bf16[8,768,4096]{2,1,0:T(8,128)(2,1)}, u32[]{:S(2)}, u32[]{:S(2)}) %all-to-all-start) | async-done | bytes 50331680 | tf_op jit(solution)/shard_map/all_to_all | solution.py:205
  2185.2 66.0 %gather_fusion.33 = bf16[2048,4096]{1,0:T(8,128)(2,1)} fusion(bf16[6144,4096]{1,0:T(8,128)(2,1)} %bitcast.20, s32[2048]{0:T(1024)S(1)} %copy-done.38), kind=kCustom, calls=%fused_computation.33 | custom fusion | bytes 33562624 | tf_op jit(solution)/shard_map/jit(_take)/gather | solution.py:222
  2251.2 65.9 %gather_fusion.32 = bf16[2048,4096]{1,0:T(8,128)(2,1)} fusion(bf16[6144,4096]{1,0:T(8,128)(2,1)} %bitcast.20, s32[2048]{0:T(1024)S(1)} %copy-done.36), kind=kCustom, calls=%fused_computation.32 | custom fusion | bytes 33562624 | tf_op jit(solution)/shard_map/jit(_take)/gather | solution.py:222
  2317.2 28.7 fusion.8
  2364.7 150.8 %fusion.120 = f32[4096,2752]{0,1:T(8,128)} fusion(bf16[6144,2752]{0,1:T(8,128)(2,1)} %get-tuple-element.25, bf16[6144,4096]{1,0:T(8,128)(2,1)} %bitcast.104), kind=kOutput, calls=%fused_computation.317 | convolution fusion | flops 138512695296 | bytes 129236992 | tf_op jit(solution)/shard_map/dot_general | solution.py:219
  2515.5 255.6 %all-to-all-done.1 = bf16[8,768,3072]{2,1,0:T(8,128)(2,1)} async-done(((bf16[8,768,3072]{2,1,0:T(8,128)(2,1)}), bf16[8,768,3072]{2,1,0:T(8,128)(2,1)}, u32[]{:S(2)}, u32[]{:S(2)}) %all-to-all-start.1) | async-done | bytes 37748768 | tf_op jit(solution)/shard_map/all_to_all | solution.py:218
  2791.8 56.8 %gather_fusion.36 = bf16[2048,3072]{1,0:T(8,128)(2,1)} fusion(bf16[6144,3072]{1,0:T(8,128)(2,1)} %bitcast.32, s32[2048]{0:T(1024)S(1)} %copy-done.37), kind=kCustom, calls=%fused_computation.36 | custom fusion | bytes 25174016 | tf_op jit(solution)/shard_map/jit(_take)/gather | solution.py:222
  2848.6 56.7 %gather_fusion.37 = bf16[2048,3072]{1,0:T(8,128)(2,1)} fusion(bf16[6144,3072]{1,0:T(8,128)(2,1)} %bitcast.32, s32[2048]{0:T(1024)S(1)} %copy-done.39), kind=kCustom, calls=%fused_computation.37 | custom fusion | bytes 25174016 | tf_op jit(solution)/shard_map/jit(_take)/gather | solution.py:222
  2905.3 19.0 shard_map.179.refs_0_
  2928.6 17.2 gather_fusion.35
  2945.9 17.2 gather_fusion.34
  (298 shorter events, 196.7 us)
Async XLA Ops:
  12.3 166.2 %collective-permute-start.22 = (f32[2,2048]{1,0:T(2,128)}, f32[2,2048]{1,0:T(2,128)}, u32[]{:S(2)}, u32[]{:S(2)}) collective-permute-start(f32[2,2048]{1,0:T(2,128)} %fusion.131), channel_id=1, source_target_pairs={{0,2},{1,3},{2,0},{3,1},{4,6},{5,7},{6,4},{7,5}} | collective-permute-start | bytes 49160 | tf_op jit(solution)/shard_map/ppermute | solution.py:121
  12.3 166.2 %collective-permute-start.27 = (f32[2,2048]{1,0:T(2,128)}, f32[2,2048]{1,0:T(2,128)}, u32[]{:S(2)}, u32[]{:S(2)}) collective-permute-start(f32[2,2048]{1,0:T(2,128)} %fusion.131), channel_id=1, source_target_pairs={{0,4},{1,5},{2,6},{3,7},{4,0},{5,1},{6,2},{7,3}} | collective-permute-start | bytes 49160 | tf_op jit(solution)/shard_map/ppermute | solution.py:121
  14.5 28.5 copy-start.60
  14.5 32.0 %copy-start.61 = (s32[2048]{0:T(1024)S(1)}, s32[2048]{0:T(1024)}, u32[]{:S(2)}) copy-start(s32[2048]{0:T(1024)} %constant.118) | copy-start | bytes 24580
  14.5 126.4 %collective-permute-start.12 = (s32[4,2048]{1,0:T(4,128)}, s32[4,2048]{1,0:T(4,128)}, u32[]{:S(2)}, u32[]{:S(2)}) collective-permute-start(s32[4,2048]{1,0:T(4,128)} %pad_add_fusion), channel_id=1, source_target_pairs={{0,4},{1,5},{2,6},{3,7},{4,0},{5,1},{6,2},{7,3}} | collective-permute-start | bytes 98312 | tf_op jit(solution)/shard_map/ppermute | solution.py:121
  14.5 127.6 %collective-permute-start.7 = (s32[4,2048]{1,0:T(4,128)}, s32[4,2048]{1,0:T(4,128)}, u32[]{:S(2)}, u32[]{:S(2)}) collective-permute-start(s32[4,2048]{1,0:T(4,128)} %pad_add_fusion), channel_id=1, source_target_pairs={{0,2},{1,3},{2,0},{3,1},{4,6},{5,7},{6,4},{7,5}} | collective-permute-start | bytes 98312 | tf_op jit(solution)/shard_map/ppermute | solution.py:121
  22.3 431.5 %collective-permute-start.11 = (bf16[2048,2048]{1,0:T(8,128)(2,1)}, bf16[2048,2048]{1,0:T(8,128)(2,1)}, u32[]{:S(2)}, u32[]{:S(2)}) collective-permute-start(bf16[2048,2048]{1,0:T(8,128)(2,1)} %get-tuple-element.65), channel_id=1, source_target_pairs={{0,4},{1,5},{2,6},{3,7},{4,0},{5,1},{6,2},{7,3}} | collective-permute-start | bytes 25165832 | tf_op jit(solution)/shard_map/ppermute | solution.py:121
  23.5 31.7 %copy-start.40 = (s32[2816]{0:T(1024)}, s32[2816]{0:T(1024)S(1)}, u32[]{:S(2)}) copy-start(s32[2816]{0:T(1024)S(1)} %fusion.87) | copy-start | bytes 33796
  68.1 75.0 %copy-start.48 = (s32[1,2048]{1,0:T(1,128)S(1)}, s32[1,2048]{1,0:T(1,128)}, u32[]{:S(2)}) copy-start(s32[1,2048]{1,0:T(1,128)} %get-tuple-element.101) | copy-start | bytes 24580
  68.1 75.0 %copy-start.45 = (s32[2048]{0:T(1024)S(1)}, s32[2048]{0:T(1024)}, u32[]{:S(2)}) copy-start(s32[2048]{0:T(1024)} %get-tuple-element.122) | copy-start | bytes 24580
  68.1 75.0 %copy-start.46 = (s32[2048]{0:T(1024)S(1)}, s32[2048]{0:T(1024)}, u32[]{:S(2)}) copy-start(s32[2048]{0:T(1024)} %get-tuple-element.123) | copy-start | bytes 24580
  68.1 75.0 %copy-start.47 = (s32[1,2048]{1,0:T(1,128)S(1)}, s32[1,2048]{1,0:T(1,128)}, u32[]{:S(2)}) copy-start(s32[1,2048]{1,0:T(1,128)} %get-tuple-element.100) | copy-start | bytes 24580
  68.1 75.1 %copy-start.65 = (s32[1,2048]{1,0:T(1,128)S(1)}, s32[1,2048]{1,0:T(1,128)}, u32[]{:S(2)}) copy-start(s32[1,2048]{1,0:T(1,128)} %get-tuple-element.103) | copy-start | bytes 24580
  68.1 78.5 %copy-start.64 = (s32[1,2048]{1,0:T(1,128)S(1)}, s32[1,2048]{1,0:T(1,128)}, u32[]{:S(2)}) copy-start(s32[1,2048]{1,0:T(1,128)} %get-tuple-element.102) | copy-start | bytes 24580
  140.9 522.1 %collective-permute-start.6 = (bf16[2048,2048]{1,0:T(8,128)(2,1)}, bf16[2048,2048]{1,0:T(8,128)(2,1)}, u32[]{:S(2)}, u32[]{:S(2)}) collective-permute-start(bf16[2048,2048]{1,0:T(8,128)(2,1)} %get-tuple-element.66), channel_id=1, source_target_pairs={{0,2},{1,3},{2,0},{3,1},{4,6},{5,7},{6,4},{7,5}} | collective-permute-start | bytes 25165832 | tf_op jit(solution)/shard_map/ppermute | solution.py:121
  161.7 40.3 %collective-permute-start = (bf16[768,2048]{1,0:T(8,128)(2,1)}, bf16[768,2048]{1,0:T(8,128)(2,1)S(1)}, u32[]{:S(2)}, u32[]{:S(2)}) collective-permute-start(bf16[768,2048]{1,0:T(8,128)(2,1)} %gather_fusion), channel_id=1, source_target_pairs={{0,1},{1,0},{2,3},{3,2},{4,5},{5,4},{6,7},{7,6}} | collective-permute-start | bytes 9437192 | tf_op jit(solution)/shard_map/ppermute | solution.py:121
  178.6 484.2 %collective-permute-start.28 = (bf16[2048,2048]{1,0:T(8,128)(2,1)}, bf16[2048,2048]{1,0:T(8,128)(2,1)}, u32[]{:S(2)}, u32[]{:S(2)}) collective-permute-start(bf16[2048,2048]{1,0:T(8,128)(2,1)} %get-tuple-element.63), channel_id=1, source_target_pairs={{0,4},{1,5},{2,6},{3,7},{4,0},{5,1},{6,2},{7,3}} | collective-permute-start | bytes 25165832 | tf_op jit(solution)/shard_map/ppermute | solution.py:121
  178.6 50.2 %collective-permute-start.3 = (bf16[768,2048]{1,0:T(8,128)(2,1)}, bf16[768,2048]{1,0:T(8,128)(2,1)}, u32[]{:S(2)}, u32[]{:S(2)}) collective-permute-start(bf16[768,2048]{1,0:T(8,128)(2,1)} %gather_fusion.4), channel_id=1, source_target_pairs={{0,1},{1,0},{2,3},{3,2},{4,5},{5,4},{6,7},{7,6}} | collective-permute-start | bytes 9437192 | tf_op jit(solution)/shard_map/ppermute | solution.py:121
  202.1 247.9 %collective-permute-start.1 = (bf16[768,2048]{1,0:T(8,128)(2,1)}, bf16[768,2048]{1,0:T(8,128)(2,1)}, u32[]{:S(2)}, u32[]{:S(2)}) collective-permute-start(bf16[768,2048]{1,0:T(8,128)(2,1)} %gather_fusion.1), channel_id=1, source_target_pairs={{0,4},{1,5},{2,6},{3,7},{4,0},{5,1},{6,2},{7,3}} | collective-permute-start | bytes 9437192 | tf_op jit(solution)/shard_map/ppermute | solution.py:121
  228.8 524.3 %collective-permute-start.23 = (bf16[2048,2048]{1,0:T(8,128)(2,1)}, bf16[2048,2048]{1,0:T(8,128)(2,1)}, u32[]{:S(2)}, u32[]{:S(2)}) collective-permute-start(bf16[2048,2048]{1,0:T(8,128)(2,1)} %get-tuple-element.64), channel_id=1, source_target_pairs={{0,2},{1,3},{2,0},{3,1},{4,6},{5,7},{6,4},{7,5}} | collective-permute-start | bytes 25165832 | tf_op jit(solution)/shard_map/ppermute | solution.py:121
  450.0 209.5 %collective-permute-start.2 = (bf16[768,2048]{1,0:T(8,128)(2,1)}, bf16[768,2048]{1,0:T(8,128)(2,1)S(1)}, u32[]{:S(2)}, u32[]{:S(2)}) collective-permute-start(bf16[768,2048]{1,0:T(8,128)(2,1)} %gather_fusion.2), channel_id=1, source_target_pairs={{0,5},{1,4},{2,7},{3,6},{4,1},{5,0},{6,3},{7,2}} | collective-permute-start | bytes 9437192 | tf_op jit(solution)/shard_map/ppermute | solution.py:121
  453.8 207.6 %collective-permute-start.4 = (bf16[768,2048]{1,0:T(8,128)(2,1)}, bf16[768,2048]{1,0:T(8,128)(2,1)}, u32[]{:S(2)}, u32[]{:S(2)}) collective-permute-start(bf16[768,2048]{1,0:T(8,128)(2,1)} %gather_fusion.5), channel_id=1, source_target_pairs={{0,2},{1,3},{2,0},{3,1},{4,6},{5,7},{6,4},{7,5}} | collective-permute-start | bytes 9437192 | tf_op jit(solution)/shard_map/ppermute | solution.py:121
  570.4 43.2 %copy-start.57 = (f32[768]{0:T(1024)S(1)}, f32[768]{0:T(1024)}, u32[]{:S(2)}) copy-start(f32[768]{0:T(1024)} %get-tuple-element.85) | copy-start | bytes 9220
  570.4 47.5 %copy-start.56 = (f32[768]{0:T(1024)S(1)}, f32[768]{0:T(1024)}, u32[]{:S(2)}) copy-start(f32[768]{0:T(1024)} %get-tuple-element.86) | copy-start | bytes 9220
  581.9 38.2 %copy-start.55 = (f32[768]{0:T(1024)S(1)}, f32[768]{0:T(1024)}, u32[]{:S(2)}) copy-start(f32[768]{0:T(1024)} %get-tuple-element.88) | copy-start | bytes 9220
  661.1 91.8 %collective-permute-start.5 = (bf16[768,2048]{1,0:T(8,128)(2,1)}, bf16[768,2048]{1,0:T(8,128)(2,1)}, u32[]{:S(2)}, u32[]{:S(2)}) collective-permute-start(bf16[768,2048]{1,0:T(8,128)(2,1)} %gather_fusion.6), channel_id=1, source_target_pairs={{0,3},{1,2},{2,1},{3,0},{4,7},{5,6},{6,5},{7,4}} | collective-permute-start | bytes 9437192 | tf_op jit(solution)/shard_map/ppermute | solution.py:121
  661.4 92.0 %collective-permute-start.13 = (bf16[768,2048]{1,0:T(8,128)(2,1)}, bf16[768,2048]{1,0:T(8,128)(2,1)}, u32[]{:S(2)}, u32[]{:S(2)}) collective-permute-start(bf16[768,2048]{1,0:T(8,128)(2,1)} %gather_fusion.12), channel_id=1, source_target_pairs={{0,1},{1,0},{2,3},{3,2},{4,5},{5,4},{6,7},{7,6}} | collective-permute-start | bytes 9437192 | tf_op jit(solution)/shard_map/ppermute | solution.py:121
  662.7 135.2 %collective-permute-start.14 = (bf16[768,2048]{1,0:T(8,128)(2,1)}, bf16[768,2048]{1,0:T(8,128)(2,1)}, u32[]{:S(2)}, u32[]{:S(2)}) collective-permute-start(bf16[768,2048]{1,0:T(8,128)(2,1)} %gather_fusion.13), channel_id=1, source_target_pairs={{0,2},{1,3},{2,0},{3,1},{4,6},{5,7},{6,4},{7,5}} | collective-permute-start | bytes 9437192 | tf_op jit(solution)/shard_map/ppermute | solution.py:121
  663.0 203.1 %collective-permute-start.15 = (bf16[768,2048]{1,0:T(8,128)(2,1)}, bf16[768,2048]{1,0:T(8,128)(2,1)}, u32[]{:S(2)}, u32[]{:S(2)}) collective-permute-start(bf16[768,2048]{1,0:T(8,128)(2,1)} %gather_fusion.14), channel_id=1, source_target_pairs={{0,3},{1,2},{2,1},{3,0},{4,7},{5,6},{6,5},{7,4}} | collective-permute-start | bytes 9437192 | tf_op jit(solution)/shard_map/ppermute | solution.py:121
  746.2 120.4 %copy-start.10 = (bf16[768,2048]{1,0:T(8,128)(2,1)S(1)}, bf16[768,2048]{1,0:T(8,128)(2,1)}, u32[]{:S(2)}) copy-start(bf16[768,2048]{1,0:T(8,128)(2,1)} %gather_fusion.28) | copy-start | bytes 9437188
  752.9 247.0 %collective-permute-start.19 = (bf16[768,2048]{1,0:T(8,128)(2,1)}, bf16[768,2048]{1,0:T(8,128)(2,1)}, u32[]{:S(2)}, u32[]{:S(2)}) collective-permute-start(bf16[768,2048]{1,0:T(8,128)(2,1)} %get-tuple-element.118), channel_id=1, source_target_pairs={{0,1},{1,0},{2,3},{3,2},{4,5},{5,4},{6,7},{7,6}} | collective-permute-start | bytes 9437192 | tf_op jit(solution)/shard_map/ppermute | solution.py:121
  753.1 247.1 %collective-permute-start.16 = (bf16[768,2048]{1,0:T(8,128)(2,1)}, bf16[768,2048]{1,0:T(8,128)(2,1)}, u32[]{:S(2)}, u32[]{:S(2)}) collective-permute-start(bf16[768,2048]{1,0:T(8,128)(2,1)} %get-tuple-element.119), channel_id=1, source_target_pairs={{0,1},{1,0},{2,3},{3,2},{4,5},{5,4},{6,7},{7,6}} | collective-permute-start | bytes 9437192 | tf_op jit(solution)/shard_map/ppermute | solution.py:121
  753.4 209.9 %collective-permute-start.8 = (bf16[768,2048]{1,0:T(8,128)(2,1)}, bf16[768,2048]{1,0:T(8,128)(2,1)}, u32[]{:S(2)}, u32[]{:S(2)}) collective-permute-start(bf16[768,2048]{1,0:T(8,128)(2,1)} %gather_fusion.8), channel_id=1, source_target_pairs={{0,1},{1,0},{2,3},{3,2},{4,5},{5,4},{6,7},{7,6}} | collective-permute-start | bytes 9437192 | tf_op jit(solution)/shard_map/ppermute | solution.py:121
  797.9 165.8 %collective-permute-start.9 = (bf16[768,2048]{1,0:T(8,128)(2,1)}, bf16[768,2048]{1,0:T(8,128)(2,1)}, u32[]{:S(2)}, u32[]{:S(2)}) collective-permute-start(bf16[768,2048]{1,0:T(8,128)(2,1)} %gather_fusion.9), channel_id=1, source_target_pairs={{0,4},{1,5},{2,6},{3,7},{4,0},{5,1},{6,2},{7,3}} | collective-permute-start | bytes 9437192 | tf_op jit(solution)/shard_map/ppermute | solution.py:121
  866.1 99.2 %collective-permute-start.10 = (bf16[768,2048]{1,0:T(8,128)(2,1)}, bf16[768,2048]{1,0:T(8,128)(2,1)}, u32[]{:S(2)}, u32[]{:S(2)}) collective-permute-start(bf16[768,2048]{1,0:T(8,128)(2,1)} %gather_fusion.10), channel_id=1, source_target_pairs={{0,5},{1,4},{2,7},{3,6},{4,1},{5,0},{6,3},{7,2}} | collective-permute-start | bytes 9437192 | tf_op jit(solution)/shard_map/ppermute | solution.py:121
  963.3 207.6 %collective-permute-start.17 = (bf16[768,2048]{1,0:T(8,128)(2,1)}, bf16[768,2048]{1,0:T(8,128)(2,1)}, u32[]{:S(2)}, u32[]{:S(2)}) collective-permute-start(bf16[768,2048]{1,0:T(8,128)(2,1)} %multiply_convert_fusion.15), channel_id=1, source_target_pairs={{0,4},{1,5},{2,6},{3,7},{4,0},{5,1},{6,2},{7,3}} | collective-permute-start | bytes 9437192 | tf_op jit(solution)/shard_map/ppermute | solution.py:121
  963.7 208.2 %collective-permute-start.18 = (bf16[768,2048]{1,0:T(8,128)(2,1)}, bf16[768,2048]{1,0:T(8,128)(2,1)}, u32[]{:S(2)}, u32[]{:S(2)}) collective-permute-start(bf16[768,2048]{1,0:T(8,128)(2,1)} %multiply_convert_fusion.14), channel_id=1, source_target_pairs={{0,5},{1,4},{2,7},{3,6},{4,1},{5,0},{6,3},{7,2}} | collective-permute-start | bytes 9437192 | tf_op jit(solution)/shard_map/ppermute | solution.py:121
  965.4 206.6 %collective-permute-start.20 = (bf16[768,2048]{1,0:T(8,128)(2,1)}, bf16[768,2048]{1,0:T(8,128)(2,1)}, u32[]{:S(2)}, u32[]{:S(2)}) collective-permute-start(bf16[768,2048]{1,0:T(8,128)(2,1)} %multiply_convert_fusion.11), channel_id=1, source_target_pairs={{0,2},{1,3},{2,0},{3,1},{4,6},{5,7},{6,4},{7,5}} | collective-permute-start | bytes 9437192 | tf_op jit(solution)/shard_map/ppermute | solution.py:121
  968.5 32.7 %copy-start.58 = (f32[2816]{0:T(1024)S(1)}, f32[2816]{0:T(1024)}, u32[]{:S(2)}) copy-start(f32[2816]{0:T(1024)} %select_maximum_fusion) | copy-start | bytes 33796
  999.9 173.1 %collective-permute-start.21 = (bf16[768,2048]{1,0:T(8,128)(2,1)}, bf16[768,2048]{1,0:T(8,128)(2,1)}, u32[]{:S(2)}, u32[]{:S(2)}) collective-permute-start(bf16[768,2048]{1,0:T(8,128)(2,1)} %multiply_convert_fusion.10), channel_id=1, source_target_pairs={{0,3},{1,2},{2,1},{3,0},{4,7},{5,6},{6,5},{7,4}} | collective-permute-start | bytes 9437192 | tf_op jit(solution)/shard_map/ppermute | solution.py:121
  1000.2 173.6 %collective-permute-start.30 = (bf16[768,2048]{1,0:T(8,128)(2,1)}, bf16[768,2048]{1,0:T(8,128)(2,1)}, u32[]{:S(2)}, u32[]{:S(2)}) collective-permute-start(bf16[768,2048]{1,0:T(8,128)(2,1)} %multiply_convert_fusion.3), channel_id=1, source_target_pairs={{0,2},{1,3},{2,0},{3,1},{4,6},{5,7},{6,4},{7,5}} | collective-permute-start | bytes 9437192 | tf_op jit(solution)/shard_map/ppermute | solution.py:121
  1170.9 31.7 %collective-permute-start.29 = (bf16[768,2048]{1,0:T(8,128)(2,1)}, bf16[768,2048]{1,0:T(8,128)(2,1)}, u32[]{:S(2)}, u32[]{:S(2)}) collective-permute-start(bf16[768,2048]{1,0:T(8,128)(2,1)} %multiply_convert_fusion.4), channel_id=1, source_target_pairs={{0,1},{1,0},{2,3},{3,2},{4,5},{5,4},{6,7},{7,6}} | collective-permute-start | bytes 9437192 | tf_op jit(solution)/shard_map/ppermute | solution.py:121
  1171.9 70.4 %collective-permute-start.31 = (bf16[768,2048]{1,0:T(8,128)(2,1)}, bf16[768,2048]{1,0:T(8,128)(2,1)}, u32[]{:S(2)}, u32[]{:S(2)}) collective-permute-start(bf16[768,2048]{1,0:T(8,128)(2,1)} %multiply_convert_fusion.2), channel_id=1, source_target_pairs={{0,3},{1,2},{2,1},{3,0},{4,7},{5,6},{6,5},{7,4}} | collective-permute-start | bytes 9437192 | tf_op jit(solution)/shard_map/ppermute | solution.py:121
  1172.0 70.2 %collective-permute-start.25 = (bf16[768,2048]{1,0:T(8,128)(2,1)}, bf16[768,2048]{1,0:T(8,128)(2,1)}, u32[]{:S(2)}, u32[]{:S(2)}) collective-permute-start(bf16[768,2048]{1,0:T(8,128)(2,1)} %multiply_convert_fusion.7), channel_id=1, source_target_pairs={{0,4},{1,5},{2,6},{3,7},{4,0},{5,1},{6,2},{7,3}} | collective-permute-start | bytes 9437192 | tf_op jit(solution)/shard_map/ppermute | solution.py:121
  1173.0 69.3 %collective-permute-start.24 = (bf16[768,2048]{1,0:T(8,128)(2,1)}, bf16[768,2048]{1,0:T(8,128)(2,1)}, u32[]{:S(2)}, u32[]{:S(2)}) collective-permute-start(bf16[768,2048]{1,0:T(8,128)(2,1)} %multiply_convert_fusion.8), channel_id=1, source_target_pairs={{0,1},{1,0},{2,3},{3,2},{4,5},{5,4},{6,7},{7,6}} | collective-permute-start | bytes 9437192 | tf_op jit(solution)/shard_map/ppermute | solution.py:121
  1173.7 135.8 %collective-permute-start.26 = (bf16[768,2048]{1,0:T(8,128)(2,1)}, bf16[768,2048]{1,0:T(8,128)(2,1)}, u32[]{:S(2)}, u32[]{:S(2)}) collective-permute-start(bf16[768,2048]{1,0:T(8,128)(2,1)} %multiply_convert_fusion.6), channel_id=1, source_target_pairs={{0,5},{1,4},{2,7},{3,6},{4,1},{5,0},{6,3},{7,2}} | collective-permute-start | bytes 9437192 | tf_op jit(solution)/shard_map/ppermute | solution.py:121
  1424.6 123.6 %copy-start.66 = (f32[1,4096]{1,0:T(1,128)S(1)}, f32[1,4096]{1,0:T(1,128)}, u32[]{:S(2)}) copy-start(f32[1,4096]{1,0:T(1,128)} %param.21) | copy-start | bytes 49156
  1635.2 550.0 %all-to-all-start = ((bf16[8,768,4096]{2,1,0:T(8,128)(2,1)}), bf16[8,768,4096]{2,1,0:T(8,128)(2,1)}, u32[]{:S(2)}, u32[]{:S(2)}) async-start(bf16[8,768,4096]{2,1,0:T(8,128)(2,1)} %bitcast.102), calls=%async_computation | async-start | bytes 100663296 | tf_op jit(solution)/shard_map/all_to_all | solution.py:205
  1810.8 374.4 %copy-start.38 = (s32[2048]{0:T(1024)S(1)}, s32[2048]{0:T(1024)}, u32[]{:S(2)}) copy-start(s32[2048]{0:T(1024)} %get-tuple-element.126) | copy-start | bytes 24580
  2185.2 66.0 %copy-start.36 = (s32[2048]{0:T(1024)S(1)}, s32[2048]{0:T(1024)}, u32[]{:S(2)}) copy-start(s32[2048]{0:T(1024)} %get-tuple-element.127) | copy-start | bytes 24580
  2251.1 66.0 %copy-start.49 = (f32[2048,1]{0,1:T(1,128)S(1)}, f32[2048,1]{0,1:T(1,128)}, u32[]{:S(2)}) copy-start(f32[2048,1]{0,1:T(1,128)} %get-tuple-element.96) | copy-start | bytes 24580
  2251.2 66.0 %copy-start.50 = (f32[2048,1]{0,1:T(1,128)S(1)}, f32[2048,1]{0,1:T(1,128)}, u32[]{:S(2)}) copy-start(f32[2048,1]{0,1:T(1,128)} %get-tuple-element.97) | copy-start | bytes 24580
  2251.2 66.0 %copy-start.62 = (pred[2048]{0:T(1024)(128)(4,1)S(1)}, pred[2048]{0:T(1024)(128)(4,1)}, u32[]{:S(2)}) copy-start(pred[2048]{0:T(1024)(128)(4,1)} %get-tuple-element.42) | copy-start | bytes 6148
  2251.2 66.0 %copy-start.63 = (pred[2048]{0:T(1024)(128)(4,1)S(1)}, pred[2048]{0:T(1024)(128)(4,1)}, u32[]{:S(2)}) copy-start(pred[2048]{0:T(1024)(128)(4,1)} %get-tuple-element.43) | copy-start | bytes 6148
  2317.1 28.7 copy-start.24
  2317.2 28.7 copy-start.26
  2317.2 28.7 copy-start.28
  2317.2 28.7 copy-start.30
  2317.2 28.9 copy-start.33
  2317.2 28.9 copy-start.35
  2356.2 414.9 %all-to-all-start.1 = ((bf16[8,768,3072]{2,1,0:T(8,128)(2,1)}), bf16[8,768,3072]{2,1,0:T(8,128)(2,1)}, u32[]{:S(2)}, u32[]{:S(2)}) async-start(bf16[8,768,3072]{2,1,0:T(8,128)(2,1)} %bitcast.105), calls=%async_computation.1 | async-start | bytes 75497472 | tf_op jit(solution)/shard_map/all_to_all | solution.py:218
  2364.7 406.4 %copy-start.21 = (f32[8,8,640]{2,1,0:T(8,128)S(1)}, f32[8,8,640]{2,1,0:T(8,128)}, u32[]{:S(2)}) copy-start(f32[8,8,640]{2,1,0:T(8,128)} %pad_maximum_fusion.4) | copy-start | bytes 491524
  2784.9 143.8 %all-to-all-start.2 = ((bf16[8,768,1024]{2,1,0:T(8,128)(2,1)}), bf16[8,768,1024]{2,1,0:T(8,128)(2,1)}, u32[]{:S(2)}, u32[]{:S(2)}) async-start(bf16[8,768,1024]{2,1,0:T(8,128)(2,1)} %bitcast.106), calls=%async_computation.2 | async-start | bytes 25165824 | tf_op jit(solution)/shard_map/all_to_all | solution.py:236
  2791.8 56.8 %copy-start.39 = (s32[2048]{0:T(1024)S(1)}, s32[2048]{0:T(1024)}, u32[]{:S(2)}) copy-start(s32[2048]{0:T(1024)} %get-tuple-element.126) | copy-start | bytes 24580
  (38 other events, 348.4 us)
